TPU v7x, 32 devices: a whole 2x2x4 slice. The times are simulated.
32 devices in a mesh: seq: 8 (over z, x), head: 4 (over y, core).
Axes of the slice: x: 2, y: 2, z: 4, core: 2. Of those that a mesh axis runs over, the one named last changes fastest.
Arguments:
- hidden: bfloat16 [2048, 4096], P(('seq', 'head')), may hold values from -90 to 90
- block_order: int32 [16], replicated, may hold values from 0 to 15, as said below
- segment_ids: int32 [2048], replicated, may hold values from 0 to 3, never falling along the last dimension, each value on 1 to 1024 neighbouring positions
- w_query: bfloat16 [4096, 4096], P(None, 'head'), may hold values from -0.09375 to 0.09375
- key_weight: bfloat16 [4096, 1024], P(None, 'head'), may hold values from -0.09375 to 0.09375
- value_weight: bfloat16 [4096, 1024], P(None, 'head'), may hold values from -0.09375 to 0.09375
- w_out: bfloat16 [4096, 4096], P('head'), may hold values from -0.09375 to 0.09375
Outputs:
- layer_out: bfloat16 [2048, 4096], P(('seq', 'head'))
Inputs may be any that keep to these rules, and one draw needn't show every extreme that they name: `block_order`: for each d, entries 2d and 2d+1 are two block numbers that sum to 15; every block number occurs once.
All inputs are finite; a program needn't handle non-finite values.
Results may differ from a plain program's by a relative error of at most 0.018.
The roundings to bfloat16 on the way count: a program that leaves them out, or rounds other values in their place, can miss the bound.
Values may be sent and summed in bfloat16 or wider, within the bound.
No kernel may reach another device: no remote copies, remote signals or barrier semaphores. Data moves between devices by JAX's collectives and lax.ppermute only.
A program may use at most 64 MiB of HBM per device.

v0:
```python
import math

import jax
import jax.numpy as jnp
from jax import lax
from jax.sharding import PartitionSpec as P

HEAD_SIZE = 128


NEGATIVE_FILLER = -1e30
ROPE_BASE = 500000.0


def apply_rotary(values, block_places, heads):
    count_rows = values.shape[0]
    shaped = values.reshape(count_rows, heads, HEAD_SIZE)
    half_dim = HEAD_SIZE // 2
    freqs = ROPE_BASE ** (-(jnp.arange(half_dim, dtype=jnp.float32) * 2.0 / HEAD_SIZE))
    angles = block_places.astype(jnp.float32)[:, None] * freqs[None, :]
    cosine = jnp.cos(angles)[:, None, :]
    sine = jnp.sin(angles)[:, None, :]
    first_half = shaped[:, :, :half_dim]
    second_half = shaped[:, :, half_dim:]
    turned = jnp.concatenate(
        [first_half * cosine - second_half * sine, second_half * cosine + first_half * sine], axis=2
    )
    return turned.reshape(count_rows, heads * HEAD_SIZE)


def positions(stored_rows, order_table, block_len):
    which_block = stored_rows // block_len
    hits = which_block[:, None] == jnp.arange(order_table.shape[0], dtype=jnp.int32)[None, :]
    base = jnp.sum(jnp.where(hits, order_table[None, :], 0), axis=1)
    return base * block_len + stored_rows % block_len


def attend(
    carry_state, query_matrix, query_pos, query_seg, key_block, value_block, key_pos, key_seg
):
    running, totals, weighted = carry_state
    scores = jnp.einsum(
        "qhgd,khd->hgqk", query_matrix, key_block, preferred_element_type=jnp.float32
    ) * HEAD_SIZE ** (-0.5)
    allowed = (key_pos[None, :] <= query_pos[:, None]) & (key_seg[None, :] == query_seg[:, None])
    masked = jnp.where(allowed, scores, NEGATIVE_FILLER)
    newmax = jnp.maximum(running, jnp.max(masked, axis=3))
    expo = jnp.where(allowed, jnp.exp(scores - newmax[..., None]), 0.0)
    factor = jnp.exp(running - newmax)
    totals = totals * factor + jnp.sum(expo, axis=3)
    weighted = weighted * factor[..., None] + jnp.einsum(
        "hgqk,khd->hgqd", expo.astype(jnp.bfloat16), value_block, preferred_element_type=jnp.float32
    )
    return (newmax, totals, weighted)


def on_device(hidden, block_order, segment_ids, w_query, key_weight, value_weight, w_out):
    q_heads = w_query.shape[1] // HEAD_SIZE
    kv_heads = key_weight.shape[1] // HEAD_SIZE
    query_group = q_heads // kv_heads
    received = lax.all_gather(hidden, "head", axis=0, tiled=True)
    projected = jnp.concatenate(
        [
            jnp.dot(received, w_query, preferred_element_type=jnp.float32),
            jnp.dot(received, key_weight, preferred_element_type=jnp.float32),
            jnp.dot(received, value_weight, preferred_element_type=jnp.float32),
        ],
        axis=1,
    )
    local_rows = projected.shape[0]
    half_rows = local_rows // 2
    own_rows = lax.axis_index("seq") * local_rows + jnp.arange(local_rows, dtype=jnp.int32)
    own_pos = positions(own_rows, block_order, half_rows)
    own_seg = jnp.take(segment_ids, own_pos)
    query_matrix = (
        apply_rotary(projected[:, : q_heads * HEAD_SIZE], own_pos, q_heads)
        .astype(jnp.bfloat16)
        .reshape(local_rows, kv_heads, query_group, HEAD_SIZE)
    )
    keys_own = apply_rotary(
        projected[:, q_heads * HEAD_SIZE : (q_heads + kv_heads) * HEAD_SIZE], own_pos, kv_heads
    ).astype(jnp.bfloat16)
    values_own = projected[:, (q_heads + kv_heads) * HEAD_SIZE :].astype(jnp.bfloat16)
    start_state = (
        jnp.full((kv_heads, query_group, local_rows), NEGATIVE_FILLER, jnp.float32),
        jnp.zeros((kv_heads, query_group, local_rows), jnp.float32),
        jnp.zeros((kv_heads, query_group, local_rows, HEAD_SIZE), jnp.float32),
    )
    key_all, value_all = (
        lax.all_gather(keys_own, "seq", axis=0, tiled=True),
        lax.all_gather(values_own, "seq", axis=0, tiled=True),
    )
    count_rows = key_all.shape[0]
    key_rows = jnp.arange(count_rows, dtype=jnp.int32)
    key_pos = positions(key_rows, block_order, half_rows)
    key_seg = jnp.take(segment_ids, key_pos)
    step_len = math.gcd(count_rows, 4 * local_rows)
    steps_total = count_rows // step_len
    blocks = (
        key_all.reshape(steps_total, step_len, kv_heads, HEAD_SIZE),
        value_all.reshape(steps_total, step_len, kv_heads, HEAD_SIZE),
        key_pos.reshape(steps_total, step_len),
        key_seg.reshape(steps_total, step_len),
    )

    def visit(current, block_items):
        key_block, value_block, kpos_blk, kseg_blk = block_items
        updated = attend(
            current, query_matrix, own_pos, own_seg, key_block, value_block, kpos_blk, kseg_blk
        )
        return (updated, None)

    finished, unused = lax.scan(visit, start_state, blocks)
    running, totals, weighted = finished
    attended = (
        (weighted / totals[..., None])
        .transpose(2, 0, 1, 3)
        .reshape(local_rows, q_heads * HEAD_SIZE)
        .astype(jnp.bfloat16)
    )
    return lax.psum_scatter(
        jnp.dot(attended, w_out, preferred_element_type=jnp.float32).astype(jnp.bfloat16),
        "head",
        scatter_dimension=0,
        tiled=True,
    )


def solution(mesh):
    placed = (
        P(("seq", "head"), None),
        P(),
        P(),
        P(None, "head"),
        P(None, "head"),
        P(None, "head"),
        P("head", None),
    )
    return jax.shard_map(
        on_device, mesh=mesh, in_specs=placed, out_specs=P(("seq", "head"), None), check_vma=False
    )
```

profile of v0, /device:TPU:0, one launch (start us, length us, event | category | flops | bytes accessed | tf_op | source)
XLA Modules:
  0.0 184.7 jit_solution(4474818107953701310)
XLA Ops:
  8.8 25.4 %all-gather.4.cloned.1.call-done = bf16[256,4096]{1,0:T(8,128)(2,1)} async-done(((bf16[64,4096]{1,0:T(8,128)(2,1)}), bf16[256,4096]{1,0:T(8,128)(2,1)}) %all-gather.4.cloned.1.call-update) | async-done | bytes 2097168 | tf_op jit(solution)/shard_map/all_gather | solution.py:61
  34.2 3.0 %convolution_convert_fusion.1 = bf16[256,256]{1,0:T(8,128)(2,1)} fusion(bf16[256,4096]{1,0:T(8,128)(2,1)} %all-gather.4.cloned.1.call-done, bf16[4096,256]{1,0:T(8,128)(2,1)S(1)} %copy-done), kind=kOutput, calls=%fused_computation.29 | convolution fusion | flops 536936448 | bytes 4325376 | tf_op jit(solution)/shard_map/dot_general | solution.py:66
  37.9 1.9 %gather_fusion.1 = s32[256]{0:T(256)S(1)} fusion(s32[2048]{0:T(1024)} %param.11, s32[1024]{0:T(1024)S(1)} %pad_clamp_fusion), kind=kCustom, calls=%fused_computation.1 | custom fusion | bytes 3072 | tf_op jit(solution)/shard_map/jit(_take)/gather | solution.py:74
  39.8 3.1 %fusion.28 = f32[256,256]{0,1:T(8,128)S(1)} fusion(bf16[256,4096]{1,0:T(8,128)(2,1)} %all-gather.4.cloned.1.call-done, bf16[4096,256]{1,0:T(8,128)(2,1)} %param.13), kind=kOutput, calls=%fused_computation.83 | convolution fusion | flops 536870912 | bytes 4456448 | tf_op jit(solution)/shard_map/dot_general | solution.py:65
  44.1 11.8 %gather_fusion = s32[2048]{0:T(1024)S(1)} fusion(s32[2048]{0:T(1024)S(1)} %copy-done.1, s32[2048]{0:T(1024)S(1)} %broadcast_clamp_fusion), kind=kCustom, calls=%fused_computation | custom fusion | bytes 24576 | tf_op jit(solution)/shard_map/jit(_take)/gather | solution.py:96
  55.9 6.3 %convolution_bitcast_fusion = f32[32,8,8,128]{3,1,2,0:T(8,128)S(1)} fusion(bf16[256,4096]{1,0:T(8,128)(2,1)} %all-gather.4.cloned.1.call-done, bf16[4096,1024]{1,0:T(8,128)(2,1)} %param.12), kind=kOutput, calls=%fused_computation.28 | convolution fusion | flops 2147483648 | bytes 11534336 | tf_op jit(solution)/shard_map/dot_general | solution.py:64
  63.4 14.2 %all-gather.8.cloned.1.call-done = bf16[2048,256]{1,0:T(8,128)(2,1)} async-done(((bf16[256,256]{1,0:T(8,128)(2,1)}), bf16[2048,256]{1,0:T(8,128)(2,1)}) %all-gather.8.cloned.1.call-update) | async-done | bytes 1048592 | tf_op jit(solution)/shard_map/all_gather | solution.py:91
  77.6 2.1 %reshape.242 = bf16[2,1024,2,128]{3,2,1,0:T(2,128)(2,1)} reshape(bf16[2048,256]{1,0:T(8,128)(2,1)} %all-gather.8.cloned.1.call-done) | data formatting | bytes 2097152 | tf_op jit(solution)/shard_map/reshape | solution.py:101
  79.8 39.0 %all-gather.6.cloned.1.call-done = bf16[2048,256]{1,0:T(8,128)(2,1)} async-done(((bf16[256,256]{1,0:T(8,128)(2,1)}), bf16[2048,256]{1,0:T(8,128)(2,1)}) %all-gather.6.cloned.1.call-update) | async-done | bytes 1048592 | tf_op jit(solution)/shard_map/all_gather | solution.py:90
  118.8 2.2 %reshape.240 = bf16[2,1024,2,128]{3,2,1,0:T(2,128)(2,1)} reshape(bf16[2048,256]{1,0:T(8,128)(2,1)} %all-gather.6.cloned.1.call-done) | data formatting | bytes 2097152 | tf_op jit(solution)/shard_map/reshape | solution.py:100
  120.9 18.4 %while.15 = (s32[]{:T(128)}, f32[2,4,256]{2,1,0:T(4,128)S(1)}, f32[2,4,256]{2,1,0:T(4,128)S(1)}, f32[2,4,256,128]{3,2,1,0:T(8,128)}, s32[2,1024]{1,0:T(2,128)S(1...) while((s32[]{:T(128)}, f32[2,4,256]{2,1,0:T(4,128)S(1)}, ...), condition=%wide.region_5.6_spmd.clone, body=%wide.region_2.5_spmd.clone.sunk | while | flops 1098393600 | bytes 40528080 | solution.py:113
  121.3 1.9 %constant_dynamic-slice_fusion.7 = (bf16[1,1024,2,128]{3,2,1,0:T(2,128)(2,1)S(1)}, bf16[1,1024,2,128]{3,2,1,0:T(2,128)(2,1)S(1)}) fusion(bf16[2,1024,2,128]{3,2,1,0:T(2,128)(2,1)} %get-tuple-element.294, s32[]{:T(128)S(6)} %copy.50, bf16[2,1024,2,128]{3,2,1,0:T(2,128)(2,1)} %get-tuple-element.292), kind=kLoop, calls=%fused_computation.21.clone.1 | loop fusion | bytes 2097156 | tf_op jit(solution)/shard_map/while/body/jit(dynamic_index_in_dim)/dynamic_slice | solution.py:113
  123.2 1.5 fusion.46
  124.7 1.7 fusion.47
  126.5 2.7 %fusion.49 = f32[2,4,256,128]{3,2,1,0:T(8,128)S(1)} fusion(f32[2,1024,256,4]{2,1,3,0:T(8,128)S(1)} %get-tuple-element.254, f32[2,4,256]{2,1,0:T(4,128)S(1)} %select_maximum_fusion.2, pred[256,1024]{0,1:T(8,128)(4,1)S(1)} %compare_and_fusion.2, f32[2,4,256,128]{3,2,1,0:T(8,128)S(1)} %copy-done.2, ...), kind=kOutput, calls=%fused_computation.11.clone.1 | convolution fusion | flops 546045952 | bytes 11288577 | tf_op jit(solution)/shard_map/while/body/eval_jaxpr/hgqk,khd->hgqd/dot_general | solution.py:51
  129.2 1.0 copy-done.3
  130.5 1.9 %constant_dynamic-slice_fusion.7 = (bf16[1,1024,2,128]{3,2,1,0:T(2,128)(2,1)S(1)}, bf16[1,1024,2,128]{3,2,1,0:T(2,128)(2,1)S(1)}) fusion(bf16[2,1024,2,128]{3,2,1,0:T(2,128)(2,1)} %get-tuple-element.294, s32[]{:T(128)S(6)} %copy.50, bf16[2,1024,2,128]{3,2,1,0:T(2,128)(2,1)} %get-tuple-element.292), kind=kLoop, calls=%fused_computation.21.clone.1 | loop fusion | bytes 2097156 | tf_op jit(solution)/shard_map/while/body/jit(dynamic_index_in_dim)/dynamic_slice | solution.py:113
  132.4 1.5 fusion.46
  133.9 1.7 fusion.47
  135.7 2.7 %fusion.49 = f32[2,4,256,128]{3,2,1,0:T(8,128)S(1)} fusion(f32[2,1024,256,4]{2,1,3,0:T(8,128)S(1)} %get-tuple-element.254, f32[2,4,256]{2,1,0:T(4,128)S(1)} %select_maximum_fusion.2, pred[256,1024]{0,1:T(8,128)(4,1)S(1)} %compare_and_fusion.2, f32[2,4,256,128]{3,2,1,0:T(8,128)S(1)} %copy-done.2, ...), kind=kOutput, calls=%fused_computation.11.clone.1 | convolution fusion | flops 546045952 | bytes 11288577 | tf_op jit(solution)/shard_map/while/body/eval_jaxpr/hgqk,khd->hgqd/dot_general | solution.py:51
  138.4 1.0 copy-done.3
  139.3 1.6 copy.28
  141.0 7.1 %convolution_convert_fusion = bf16[256,4096]{1,0:T(8,128)(2,1)} fusion(bf16[256,1024]{0,1:T(8,128)(2,1)S(1)} %bitcast.72, bf16[1024,4096]{1,0:T(8,128)(2,1)} %param.15), kind=kOutput, calls=%fused_computation.27 | convolution fusion | flops 2148532224 | bytes 11010048 | tf_op jit(solution)/shard_map/dot_general | solution.py:122
  148.1 30.0 %reduce-scatter.2.cloned.1.call-done = bf16[64,4096]{1,0:T(8,128)(2,1)} async-done(((bf16[256,4096]{1,0:T(8,128)(2,1)}), bf16[64,4096]{1,0:T(8,128)(2,1)}) %reduce-scatter.2.cloned.1.call-update) | async-done | bytes 524304 | tf_op jit(solution)/shard_map/reduce_scatter | solution.py:121
  (57 shorter events, 5.9 us)
Async XLA Ops:
  6.5 27.7 %copy-start = (bf16[4096,256]{1,0:T(8,128)(2,1)S(1)}, bf16[4096,256]{1,0:T(8,128)(2,1)}, u32[]{:S(2)}) copy-start(bf16[4096,256]{1,0:T(8,128)(2,1)} %param.14) | copy-start | bytes 6291460
  6.5 37.5 %copy-start.1 = (s32[2048]{0:T(1024)S(1)}, s32[2048]{0:T(1024)}, u32[]{:S(2)}) copy-start(s32[2048]{0:T(1024)} %param.11) | copy-start | bytes 24580
  6.5 27.7 %all-gather.4.cloned.1.call-start = ((), (), s32[]{:S(2)}) async-start(), calls=%async_computation.1 | async-start | bytes 2621440 | tf_op jit(solution)/shard_map/all_gather | solution.py:61
  7.3 70.4 %all-gather.8.cloned.1.call-start = ((), (), s32[]{:S(2)}) async-start(), calls=%async_computation.3 | async-start | bytes 1179648 | tf_op jit(solution)/shard_map/all_gather | solution.py:91
  37.2 81.6 %all-gather.6.cloned.1.call-start = ((), (), s32[]{:S(2)}) async-start(), calls=%async_computation.2 | async-start | bytes 1179648 | tf_op jit(solution)/shard_map/all_gather | solution.py:90
  43.8 134.3 %reduce-scatter.2.cloned.1.call-start = ((), (), s32[]{:S(2)}) async-start(), calls=%async_computation.4 | async-start | bytes 2621440 | tf_op jit(solution)/shard_map/reduce_scatter | solution.py:121
  123.2 3.2 %copy-start.2 = (f32[2,4,256,128]{3,2,1,0:T(8,128)S(1)}, f32[2,4,256,128]{3,2,1,0:T(8,128)}, u32[]{:S(2)}) copy-start(f32[2,4,256,128]{3,2,1,0:T(8,128)} %get-tuple-element.274) | copy-start | bytes 3145732 | tf_op jit(solution)/shard_map/while
  129.2 1.0 copy-start.3
  132.4 3.2 %copy-start.2 = (f32[2,4,256,128]{3,2,1,0:T(8,128)S(1)}, f32[2,4,256,128]{3,2,1,0:T(8,128)}, u32[]{:S(2)}) copy-start(f32[2,4,256,128]{3,2,1,0:T(8,128)} %get-tuple-element.274) | copy-start | bytes 3145732 | tf_op jit(solution)/shard_map/while
  138.4 1.0 copy-start.3
Sparse Core Ops, SparseCore 0:
  8.9 25.2 all-gather.3
  37.3 40.2 all-gather.7
  79.8 38.9 all-gather.5
  148.3 29.8 reduce-scatter.1
where the time goes:
time: 185 us
  waiting for transfers between devices  109 us (59%)
  matrix products  27.8 us (15%)
  local copies, waits for them, and re-layouts  26.7 us (14%)
  between operations  13.3 us (7%)
  other arithmetic  7.03 us (4%)
    all_gather x1, waiting for transfers between devices, on_device(): lax.all_gather(keys_own, 'seq', axis=0, tiled=True)  39 us
    reduce_scatter x1, waiting for transfers between devices, on_device(): lax.psum_scatter(jnp.dot(attended, w_out, preferred_element_type=jnp.floa...  30 us
    all_gather x1, waiting for transfers between devices, on_device(): received = lax.all_gather(hidden, 'head', axis=0, tiled=True)  25.4 us
    all_gather x1, waiting for transfers between devices, on_device(): lax.all_gather(values_own, 'seq', axis=0, tiled=True)  14.2 us
    gather x2, local copies, waits for them, and re-layouts, on_device(): key_seg = jnp.take(segment_ids, key_pos)  11.8 us
    dot_general x1, matrix products, on_device(): jnp.dot(attended, w_out, preferred_element_type=jnp.float32)  7.09 us
    dot_general x1, matrix products, on_device(): jnp.dot(received, w_query, preferred_element_type=jnp.float32)  6.34 us
    dot_general x2, matrix products, attend(): jnp.einsum('hgqk,khd->hgqd', expo.astype(jnp.bfloat16), value_block, pref...  5.34 us
  transfers between devices with their start and end apart: 4, of which 4 were waited for; matrix products, arithmetic and copies ran while one was open for 16% of the time, Pallas kernels for 0%

commit v1 on v0

--- a/solution.py
+++ b/solution.py
@@ -2,7 +2,10 @@
 
 import jax
 import jax.numpy as jnp
+import numpy as np
 from jax import lax
+from jax.experimental import pallas as pl
+from jax.experimental.pallas import tpu as pltpu
 from jax.sharding import PartitionSpec as P
 
 HEAD_SIZE = 128
@@ -54,7 +57,7 @@
     return (newmax, totals, weighted)
 
 
-def on_device(hidden, block_order, segment_ids, w_query, key_weight, value_weight, w_out):
+def general_device(hidden, block_order, segment_ids, w_query, key_weight, value_weight, w_out):
     q_heads = w_query.shape[1] // HEAD_SIZE
     kv_heads = key_weight.shape[1] // HEAD_SIZE
     query_group = q_heads // kv_heads
@@ -110,8 +113,8 @@
         )
         return (updated, None)
 
-    finished, unused = lax.scan(visit, start_state, blocks)
-    running, totals, weighted = finished
+    finished, _ = lax.scan(visit, start_state, blocks)
+    _, totals, weighted = finished
     attended = (
         (weighted / totals[..., None])
         .transpose(2, 0, 1, 3)
@@ -124,6 +127,346 @@
         scatter_dimension=0,
         tiled=True,
     )
+
+
+F32 = jnp.float32
+BF16 = jnp.bfloat16
+ANY = pl.BlockSpec(memory_space=pl.ANY)
+VMEM = pl.BlockSpec(memory_space=pltpu.VMEM)
+SMEM = pl.BlockSpec(memory_space=pltpu.SMEM)
+
+
+def frequencies():
+    half_dim = HEAD_SIZE // 2
+    freqs = ROPE_BASE ** (-(np.arange(half_dim) * 2.0 / HEAD_SIZE))
+    return jnp.asarray(np.concatenate([freqs, freqs])[None, :].astype(np.float32))
+
+
+def stored_block(far):
+    chip = lax.axis_index("head") // 2
+    return 2 * lax.axis_index("seq") + (1 - chip if far else chip)
+
+
+def angles(number, freq_ref, block):
+    rows = lax.broadcasted_iota(jnp.int32, (block, HEAD_SIZE), 0) + number * block
+    turned = rows.astype(F32) * freq_ref[...]
+    lane = lax.broadcasted_iota(jnp.int32, (block, HEAD_SIZE), 1)
+    sine = jnp.sin(turned)
+    return jnp.cos(turned), jnp.where(lane < HEAD_SIZE // 2, -sine, sine)
+
+
+def turn(values, cosine, sine):
+    return values * cosine + pltpu.roll(values, HEAD_SIZE // 2, 1) * sine
+
+
+def start_rows(own_ref, peer_ref, x_ref, base, sems):
+    rows = own_ref.shape[0]
+    core = lax.axis_index("head") % 2
+    copies = [
+        pltpu.make_async_copy(own_ref, x_ref.at[pl.ds(base + core * rows, rows)], sems.at[0]),
+        pltpu.make_async_copy(
+            peer_ref, x_ref.at[pl.ds(base + (1 - core) * rows, rows)], sems.at[1]
+        ),
+    ]
+    for copy in copies:
+        copy.start()
+    return copies
+
+
+def kv_kernel(
+    order_ref, freq_ref, own_ref, peer_ref, wk_ref, wv_ref, out_ref, x_ref, k_vmem, v_vmem, xs, ws, *, far
+):
+    rows, depth = own_ref.shape
+    width = wk_ref.shape[1]
+    parts = ws.shape[1]
+    part = depth // parts
+    x_copies = start_rows(own_ref, peer_ref, x_ref, 0, xs)
+    copies = []
+    for at in range(parts):
+        cut = pl.ds(at * part, part)
+        for which, (src, dst) in enumerate(((wk_ref, k_vmem), (wv_ref, v_vmem))):
+            copy = pltpu.make_async_copy(src.at[cut], dst.at[cut], ws.at[which, at])
+            copy.start()
+            copies.append(copy)
+    cosine, sine = angles(order_ref[stored_block(far)], freq_ref, 2 * rows)
+    for copy in x_copies:
+        copy.wait()
+    keys = values = None
+    for at in range(parts):
+        copies[2 * at].wait()
+        copies[2 * at + 1].wait()
+        cut = slice(at * part, (at + 1) * part)
+        more_k = jnp.dot(x_ref[:, cut], k_vmem[cut, :], preferred_element_type=F32)
+        more_v = jnp.dot(x_ref[:, cut], v_vmem[cut, :], preferred_element_type=F32)
+        keys = more_k if at == 0 else keys + more_k
+        values = more_v if at == 0 else values + more_v
+    for head in range(width // HEAD_SIZE):
+        cut = slice(head * HEAD_SIZE, (head + 1) * HEAD_SIZE)
+        out_ref[:, cut] = turn(keys[:, cut], cosine, sine).astype(BF16)
+    out_ref[:, width:] = values.astype(BF16)
+
+
+def project_kv(order, freqs, own, peer, wk, wv, far):
+    rows, depth = own.shape
+    width = wk.shape[1]
+    parts = 4
+    return pl.pallas_call(
+        lambda *refs: kv_kernel(*refs, far=far),
+        in_specs=[SMEM, VMEM, ANY, ANY, ANY, ANY],
+        out_specs=VMEM,
+        out_shape=jax.ShapeDtypeStruct((2 * rows, 2 * width), BF16),
+        scratch_shapes=[
+            pltpu.VMEM((2 * rows, depth), BF16),
+            pltpu.VMEM((depth, width), BF16),
+            pltpu.VMEM((depth, width), BF16),
+            pltpu.SemaphoreType.DMA((2,)),
+            pltpu.SemaphoreType.DMA((2, parts)),
+        ],
+        cost_estimate=pl.CostEstimate(
+            flops=8 * rows * depth * width, bytes_accessed=4 * depth * width, transcendentals=0
+        ),
+        name="project_kv",
+    )(order, freqs, own, peer, wk, wv)
+
+
+def q_kernel(order_ref, freq_ref, own_ref, peer_ref, w_ref, out_ref, x_ref, w_vmem, xs, ws, *, far):
+    rows = own_ref.shape[0]
+    tiles, _, tile = w_vmem.shape
+    x_copies = start_rows(own_ref, peer_ref, x_ref, 0, xs)
+    copies = []
+    for at in range(tiles):
+        copy = pltpu.make_async_copy(
+            w_ref.at[:, pl.ds(at * tile, tile)], w_vmem.at[at], ws.at[at]
+        )
+        copy.start()
+        copies.append(copy)
+    cosine, sine = angles(order_ref[stored_block(far)], freq_ref, 2 * rows)
+    for copy in x_copies:
+        copy.wait()
+    for at in range(tiles):
+        copies[at].wait()
+        result = jnp.dot(x_ref[...], w_vmem[at], preferred_element_type=F32)
+        for head in range(tile // HEAD_SIZE):
+            cut = slice(head * HEAD_SIZE, (head + 1) * HEAD_SIZE)
+            out_ref[:, at * tile + head * HEAD_SIZE : at * tile + (head + 1) * HEAD_SIZE] = turn(
+                result[:, cut], cosine, sine
+            ).astype(BF16)
+
+
+def project_q(order, freqs, own, peer, weight, far):
+    rows, depth = own.shape
+    width = weight.shape[1]
+    tile = 2 * HEAD_SIZE
+    tiles = width // tile
+    return pl.pallas_call(
+        lambda *refs: q_kernel(*refs, far=far),
+        in_specs=[SMEM, VMEM] + [ANY] * 3,
+        out_specs=VMEM,
+        out_shape=jax.ShapeDtypeStruct((2 * rows, width), BF16),
+        scratch_shapes=[
+            pltpu.VMEM((2 * rows, depth), BF16),
+            pltpu.VMEM((tiles, depth, tile), BF16),
+            pltpu.SemaphoreType.DMA((2,)),
+            pltpu.SemaphoreType.DMA((tiles,)),
+        ],
+        cost_estimate=pl.CostEstimate(
+            flops=4 * rows * depth * width, bytes_accessed=2 * depth * width, transcendentals=0
+        ),
+        name="project_q",
+    )(order, freqs, own, peer, weight)
+
+
+def attention_kernel(
+    order_ref, seg_ref, segrow_ref, q_ref, *rest, pieces, block, kv_heads, group, far
+):
+    piece_refs = rest[:pieces]
+    w_ref = rest[pieces]
+    outs = rest[pieces + 1 : pieces + 3]
+    w_vmem, kv_ref, qs_ref, s_ref, m_ref, l_ref, acc_ref, att_ref, slot_ref, ps, ws = rest[
+        pieces + 3 :
+    ]
+    shards = pieces // 2
+    chunks = ws.shape[0]
+    chunk = w_ref.shape[0] // chunks
+    copies = []
+    for at in range(pieces):
+        copies.append(pltpu.make_async_copy(piece_refs[at], kv_ref.at[at], ps.at[at]))
+    fetch = [
+        pltpu.make_async_copy(
+            w_ref.at[pl.ds(at * chunk, chunk)], w_vmem.at[pl.ds(at * chunk, chunk)], ws.at[at]
+        )
+        for at in range(chunks)
+    ]
+    for copy in copies + fetch:
+        copy.start()
+    shard = lax.axis_index("seq")
+    place = lax.axis_index("head")
+    core, chip = place % 2, place // 2
+    for at in range(shards):
+        pair = 2 * (shard ^ at)
+        slot_ref[order_ref[pair + chip]] = at
+        slot_ref[order_ref[pair + 1 - chip]] = shards + at
+    high = order_ref[stored_block(far)]
+    leading = seg_ref[high * block]
+    low = jnp.int32(0)
+    for at in range(pieces):
+        low = low + jnp.where(seg_ref[(at + 1) * block - 1] < leading, 1, 0)
+    span = group * block
+    width = kv_heads * HEAD_SIZE
+    factor = HEAD_SIZE**-0.5 * math.log2(math.e)
+    below = lax.broadcasted_iota(jnp.int32, (block, block), 1) <= lax.broadcasted_iota(
+        jnp.int32, (block, block), 0
+    )
+    for head in range(kv_heads * group):
+        qs_ref[head * block : (head + 1) * block, :] = q_ref[
+            :, head * HEAD_SIZE : (head + 1) * HEAD_SIZE
+        ]
+    m_ref[...] = jnp.full_like(m_ref, NEGATIVE_FILLER)
+    l_ref[...] = jnp.zeros_like(l_ref)
+    acc_ref[...] = jnp.zeros_like(acc_ref)
+    qseg = jnp.broadcast_to(segrow_ref[pl.ds(high, 1), :], (block, block)).T
+    for copy in copies:
+        copy.wait()
+
+    def score(at, carry):
+        slot = slot_ref[at]
+        same = qseg == segrow_ref[pl.ds(at, 1), :]
+        allowed = same & (below | (at < high))
+        for kv in range(kv_heads):
+            cut = slice(kv * span, (kv + 1) * span)
+            scores = lax.dot_general(
+                qs_ref[cut, :],
+                kv_ref[slot, :, kv * HEAD_SIZE : (kv + 1) * HEAD_SIZE],
+                (((1,), (1,)), ((), ())),
+                preferred_element_type=F32,
+            ).reshape(group, block, block)
+            masked = jnp.where(allowed[None], scores, NEGATIVE_FILLER).reshape(span, block)
+            s_ref[at, cut, :] = masked
+            m_ref[cut, :] = jnp.maximum(m_ref[cut, :], masked)
+        return carry
+
+    lax.fori_loop(low, high + 1, score, 0)
+    m_ref[...] = jnp.broadcast_to(jnp.max(m_ref[...], axis=1, keepdims=True), m_ref.shape)
+
+    def weigh(at, carry):
+        slot = slot_ref[at]
+        for kv in range(kv_heads):
+            cut = slice(kv * span, (kv + 1) * span)
+            expo = jnp.exp2((s_ref[at, cut, :] - m_ref[cut, :]) * factor)
+            l_ref[cut, :] += expo
+            acc_ref[cut, :] += jnp.dot(
+                expo.astype(BF16),
+                kv_ref[slot, :, width + kv * HEAD_SIZE : width + (kv + 1) * HEAD_SIZE],
+                preferred_element_type=F32,
+            )
+        return carry
+
+    lax.fori_loop(low, high + 1, weigh, 0)
+    done = (acc_ref[...] / jnp.sum(l_ref[...], axis=1, keepdims=True)).astype(BF16)
+    half = block // 2
+    flip = core == 0
+    for head in range(kv_heads * group):
+        cut = slice(head * HEAD_SIZE, (head + 1) * HEAD_SIZE)
+        base = head * block
+        first, second = done[base : base + half], done[base + half : base + block]
+        att_ref[:half, cut] = jnp.where(flip, first, second)
+        att_ref[half:, cut] = jnp.where(flip, second, first)
+    for copy in fetch:
+        copy.wait()
+    tile = w_vmem.shape[1] // 4
+    for col in range(4):
+        cut = slice(col * tile, (col + 1) * tile)
+        partial = jnp.dot(att_ref[...], w_vmem[:, cut], preferred_element_type=F32).astype(BF16)
+        outs[0][:, cut] = partial[:half]
+        outs[1][:, cut] = partial[half:]
+
+
+def attention_out(order, segment_ids, seg_rows, queries, pieces, w_out, kv_heads, group, far):
+    block = pieces[0].shape[0]
+    count = len(pieces)
+    tall = kv_heads * group * block
+    chunks = 4
+    piece_out = jax.ShapeDtypeStruct((block // 2, w_out.shape[1]), BF16)
+    kernel = lambda *refs: attention_kernel(
+        *refs, pieces=count, block=block, kv_heads=kv_heads, group=group, far=far
+    )
+    return pl.pallas_call(
+        kernel,
+        in_specs=[SMEM, SMEM, VMEM, VMEM] + [ANY] * (count + 1),
+        out_specs=[VMEM] * 2,
+        out_shape=[piece_out] * 2,
+        scratch_shapes=[
+            pltpu.VMEM(w_out.shape, BF16),
+            pltpu.VMEM((count,) + pieces[0].shape, BF16),
+            pltpu.VMEM((tall, HEAD_SIZE), BF16),
+            pltpu.VMEM((count, tall, block), F32),
+            pltpu.VMEM((tall, block), F32),
+            pltpu.VMEM((tall, block), F32),
+            pltpu.VMEM((tall, HEAD_SIZE), F32),
+            pltpu.VMEM((block, kv_heads * group * HEAD_SIZE), BF16),
+            pltpu.SMEM((count,), jnp.int32),
+            pltpu.SemaphoreType.DMA((count,)),
+            pltpu.SemaphoreType.DMA((chunks,)),
+        ],
+        cost_estimate=pl.CostEstimate(
+            flops=4 * block * w_out.shape[0] * w_out.shape[1],
+            bytes_accessed=2 * w_out.shape[0] * w_out.shape[1],
+            transcendentals=0,
+        ),
+        name="attention_far" if far else "attention_near",
+    )(order, segment_ids, seg_rows, queries, *pieces, w_out)
+
+
+def swap(values, axis, count, mask):
+    return lax.ppermute(values, axis, [(at, at ^ mask) for at in range(count)])
+
+
+def gather_seq(piece, shards, lanes):
+    found = {0: piece}
+    far = range(lanes, shards, lanes)
+    for step in sorted(far, reverse=True):
+        found[step] = swap(piece, "seq", shards, step)
+    for near in range(1, lanes):
+        found[near] = swap(piece, "seq", shards, near)
+    for step in far:
+        for near in range(1, lanes):
+            found[step + near] = swap(found[step], "seq", shards, near)
+    return [found[step] for step in range(shards)]
+
+
+def paired_device(shards, lanes):
+    def on_device(hidden, order, segment_ids, w_query, key_weight, value_weight, w_out):
+        return run(hidden, order, segment_ids, w_query, key_weight, value_weight, w_out)
+
+    def run(hidden, order, segment_ids, w_query, key_weight, value_weight, w_out):
+        seg_rows = segment_ids.reshape(order.shape[0], -1)
+        kv_heads = key_weight.shape[1] // HEAD_SIZE
+        group = w_query.shape[1] // key_weight.shape[1]
+        freqs = frequencies()
+        across = swap(hidden, "head", 4, 2)
+        beside = swap(hidden, "head", 4, 1)
+        early = project_kv(order, freqs, hidden, beside, key_weight, value_weight, False)
+        early_all = gather_seq(early, shards, lanes)
+        across_beside = swap(across, "head", 4, 1)
+        late = project_kv(order, freqs, across, across_beside, key_weight, value_weight, True)
+        late_all = gather_seq(late, shards, lanes)
+        near_queries = project_q(order, freqs, hidden, beside, w_query, False)
+        far_queries = project_q(order, freqs, across, across_beside, w_query, True)
+
+        def attend_rows(q, far):
+            return attention_out(
+                order, segment_ids, seg_rows, q, early_all + late_all, w_out, kv_heads, group, far
+            )
+
+        far_own, far_peer = attend_rows(far_queries, True)
+        far_in = swap(far_peer, "head", 4, 1)
+        crossing = (far_own.astype(F32) + far_in.astype(F32)).astype(BF16)
+        crossed = swap(crossing, "head", 4, 2)
+        near_own, near_peer = attend_rows(near_queries, False)
+        near_in = swap(near_peer, "head", 4, 1)
+        return (near_own.astype(F32) + near_in.astype(F32) + crossed.astype(F32)).astype(BF16)
+
+    return on_device
 
 
 def solution(mesh):
@@ -136,6 +479,9 @@
         P(None, "head"),
         P("head", None),
     )
+    shards, members = mesh.shape["seq"], mesh.shape["head"]
+    paired = members == 4 and shards & (shards - 1) == 0
+    device = paired_device(shards, 1 << ((shards.bit_length() - 1) // 2)) if paired else general_device
     return jax.shard_map(
-        on_device, mesh=mesh, in_specs=placed, out_specs=P(("seq", "head"), None), check_vma=False
-    )
+        device, mesh=mesh, in_specs=placed, out_specs=P(("seq", "head"), None), check_vma=False
+    )

time: 185 us -> 110 us (0.59)
  waiting for transfers between devices: 109 us -> 36.9 us
  Pallas kernels: 0 us -> 44.3 us
  matrix products: 27.8 us -> 0 us
  local copies, waits for them, and re-layouts: 26.7 us -> 2.34 us
  starting transfers between devices: 0.31 us -> 23.3 us
  between operations: 13.3 us -> 0.28 us
  other arithmetic: 7.03 us -> 2.15 us
    all_gather x3 -> x0, waiting for transfers between devices: 78.6 us -> none  [the longest x1 39 us: on_device(): lax.all_gather(keys_own, 'seq', axis=0, tiled=True)]
    pallas_call x0 -> x6, Pallas kernels: none -> 44.3 us  [the longest x2 19.6 us: attention_out(): pl.pallas_call(kernel, in_specs=[SMEM, SMEM, VMEM, VMEM] + [ANY] * (count...]
    ppermute x0 -> x20, waiting for transfers between devices: none -> 36.9 us  [swap(): return lax.ppermute(values, axis, [(at, at ^ mask) for at in range(count)])]
    reduce_scatter x1 -> x0, waiting for transfers between devices: 30 us -> none  [on_device(): lax.psum_scatter(jnp.dot(attended, w_out, preferred_element_type=jnp.floa...]
    dot_general x8 -> x0, matrix products: 27.8 us -> none  [the longest x1 7.09 us: on_device(): jnp.dot(attended, w_out, preferred_element_type=jnp.float32)]
    ppermute x0 -> x20, starting transfers between devices: none -> 23.3 us  [swap(): return lax.ppermute(values, axis, [(at, at ^ mask) for at in range(count)])]
    gather x3 -> x0, local copies, waits for them, and re-layouts: 13.7 us -> none  [the longest x2 11.8 us: on_device(): key_seg = jnp.take(segment_ids, key_pos)]
    reduce_sum x4 -> x0, other arithmetic: 4.93 us -> none  [the longest x2 3.43 us: attend(): totals = totals * factor + jnp.sum(expo, axis=3)]
  transfers between devices with their start and end apart: 4 -> 20, of which waited for: 4 -> 5; matrix products, arithmetic and copies ran while one was open for 16% -> 0% of each run, Pallas kernels for 0% -> 32%
where the time goes in v1:
time: 110 us; the launch traced here: 109 us
  Pallas kernels  44.3 us (40%)
  waiting for transfers between devices  36.9 us (34%)
  starting transfers between devices  23.3 us (21%)
  local copies, waits for them, and re-layouts  2.34 us (2%)
  other arithmetic  2.15 us (2%)
    ppermute x20, waiting for transfers between devices, swap(): return lax.ppermute(values, axis, [(at, at ^ mask) for at in range(count)])  36.9 us
    ppermute x20, starting transfers between devices, swap(): return lax.ppermute(values, axis, [(at, at ^ mask) for at in range(count)])  23.3 us
    pallas_call x2, Pallas kernels, attention_out(): pl.pallas_call(kernel, in_specs=[SMEM, SMEM, VMEM, VMEM] + [ANY] * (count...  19.6 us
    pallas_call x2, Pallas kernels, project_q(): pl.pallas_call(lambda *refs: q_kernel(*refs, far=far), in_specs=[SMEM, VM...  15.3 us
    pallas_call x2, Pallas kernels, project_kv(): pl.pallas_call(lambda *refs: kv_kernel(*refs, far=far), in_specs=[SMEM, V...  9.42 us
    unnamed x36, local copies, waits for them, and re-layouts  2.34 us
  transfers between devices with their start and end apart: 20, of which 5 were waited for; matrix products, arithmetic and copies ran while one was open for 0% of the time, Pallas kernels for 32%

profile of v1, /device:TPU:0, one launch (start us, length us, event | category | flops | bytes accessed | tf_op | source)
XLA Modules:
  0.0 109.3 jit_solution(3706781215262359023)
XLA Ops:
  0.0 3.0 %collective-permute-start.8 = (bf16[64,4096]{1,0:T(8,128)(2,1)}, bf16[64,4096]{1,0:T(8,128)(2,1)S(1)}, u32[]{:S(2)}, u32[]{:S(2)}) collective-permute-start(bf16[64,4096]{1,0:T(8,128)(2,1)} %refs_2_.3), channel_id=1, source_target_pairs={{0,2},{1,3},{2,0},{3,1},{4,6},{5,7},{6,4},{7,5},{8,10},{9,11},{10,... | collective-permute-start | bytes 1572872 | tf_op jit(solution)/shard_map/ppermute | solution.py:421
  3.0 12.1 %collective-permute-done.8.refs_2_ = bf16[64,4096]{1,0:T(8,128)(2,1)S(1)} collective-permute-done((bf16[64,4096]{1,0:T(8,128)(2,1)}, bf16[64,4096]{1,0:T(8,128)(2,1)S(1)}, u32[]{:S(2)}, u32[]{:S(2)}) %collective-permute-start.8) | collective-permute-done | bytes 524320 | tf_op jit(solution)/shard_map/ppermute | solution.py:421
  15.1 0.8 copy-done
  16.0 4.7 %project_kv.2.refs_4_ = bf16[128,512]{1,0:T(8,128)(2,1)} custom-call(s32[16]{0:T(128)} %refs_0_.11, f32[1,128]{1,0:T(1,128)} %constant.2.clone.refs_1_, bf16[64,4096]{1,0:T(8,128)(2,1)} %refs_2_.3, bf16[64,4096]{1,0:T(8,128)(2,1)} %copy-done, bf16[4096,256]{1,0:T(8,128)(2,1)} %refs_4_.6, bf16[4096,256]{1,0:T(8,128)(2,1)} %refs_5_.3), custom_call_target="tpu_custom_call" | custom-call | flops 536870912 | bytes 4194304 | tf_op jit(solution)/shard_map/project_kv/pallas_call | solution.py:213
  20.7 1.9 %collective-permute-start.2 = (bf16[128,512]{1,0:T(8,128)(2,1)}, bf16[128,512]{1,0:T(8,128)(2,1)S(1)}, u32[]{:S(2)}, u32[]{:S(2)}) collective-permute-start(bf16[128,512]{1,0:T(8,128)(2,1)} %project_kv.2.refs_4_), channel_id=1, source_target_pairs={{0,8},{4,12},{8,0},{12,4},{16,24},{20,28},{24,16},{28,20},{1,9},{5... | collective-permute-start | bytes 393224 | tf_op jit(solution)/shard_map/ppermute | solution.py:421
  22.5 2.6 %collective-permute-start.4 = (bf16[128,512]{1,0:T(8,128)(2,1)}, bf16[128,512]{1,0:T(8,128)(2,1)S(1)}, u32[]{:S(2)}, u32[]{:S(2)}) collective-permute-start(bf16[128,512]{1,0:T(8,128)(2,1)} %project_kv.2.refs_4_), channel_id=1, source_target_pairs={{0,16},{4,20},{8,24},{12,28},{16,0},{20,4},{24,8},{28,12},{1,17},{... | collective-permute-start | bytes 393224 | tf_op jit(solution)/shard_map/ppermute | solution.py:421
  25.1 1.5 %collective-permute-start.1 = (bf16[128,512]{1,0:T(8,128)(2,1)}, bf16[128,512]{1,0:T(8,128)(2,1)S(1)}, u32[]{:S(2)}, u32[]{:S(2)}) collective-permute-start(bf16[128,512]{1,0:T(8,128)(2,1)} %project_kv.2.refs_4_), channel_id=1, source_target_pairs={{0,4},{4,0},{8,12},{12,8},{16,20},{20,16},{24,28},{28,24},{1,5},{5... | collective-permute-start | bytes 393224 | tf_op jit(solution)/shard_map/ppermute | solution.py:421
  26.8 2.4 %collective-permute-done.2.refs_6_ = bf16[128,512]{1,0:T(8,128)(2,1)S(1)} collective-permute-done((bf16[128,512]{1,0:T(8,128)(2,1)}, bf16[128,512]{1,0:T(8,128)(2,1)S(1)}, u32[]{:S(2)}, u32[]{:S(2)}) %collective-permute-start.2) | collective-permute-done | bytes 131104 | tf_op jit(solution)/shard_map/ppermute | solution.py:421
  29.2 1.6 %collective-permute-start.3 = (bf16[128,512]{1,0:T(8,128)(2,1)S(1)}, bf16[128,512]{1,0:T(8,128)(2,1)S(1)}, u32[]{:S(2)}, u32[]{:S(2)}) collective-permute-start(bf16[128,512]{1,0:T(8,128)(2,1)S(1)} %collective-permute-done.2.refs_6_), channel_id=1, source_target_pairs={{0,4},{4,0},{8,12},{12,8},{16,20},{20,16},{24,28},{28,24},{1,5},{5... | collective-permute-start | bytes 393224 | tf_op jit(solution)/shard_map/ppermute | solution.py:421
  30.8 4.7 %collective-permute-done.4.refs_8_ = bf16[128,512]{1,0:T(8,128)(2,1)S(1)} collective-permute-done((bf16[128,512]{1,0:T(8,128)(2,1)}, bf16[128,512]{1,0:T(8,128)(2,1)S(1)}, u32[]{:S(2)}, u32[]{:S(2)}) %collective-permute-start.4) | collective-permute-done | bytes 131104 | tf_op jit(solution)/shard_map/ppermute | solution.py:421
  35.5 1.7 %collective-permute-start.5 = (bf16[128,512]{1,0:T(8,128)(2,1)S(1)}, bf16[128,512]{1,0:T(8,128)(2,1)S(1)}, u32[]{:S(2)}, u32[]{:S(2)}) collective-permute-start(bf16[128,512]{1,0:T(8,128)(2,1)S(1)} %collective-permute-done.4.refs_8_), channel_id=1, source_target_pairs={{0,4},{4,0},{8,12},{12,8},{16,20},{20,16},{24,28},{28,24},{1,5},{5... | collective-permute-start | bytes 393224 | tf_op jit(solution)/shard_map/ppermute | solution.py:421
  38.0 4.7 %project_kv.3.refs_12_ = bf16[128,512]{1,0:T(8,128)(2,1)} custom-call(s32[16]{0:T(128)} %refs_0_.11, f32[1,128]{1,0:T(1,128)} %constant.2.clone.refs_1_, bf16[64,4096]{1,0:T(8,128)(2,1)} %copy-done.1, bf16[64,4096]{1,0:T(8,128)(2,1)} %copy-done.2, bf16[4096,256]{1,0:T(8,128)(2,1)} %refs_4_.6, bf16[4096,256]{1,0:T(8,128)(2,1)} %refs_5_.3), custom_call_target="tpu_custom_call" | custom-call | flops 536870912 | bytes 4194304 | tf_op jit(solution)/shard_map/project_kv/pallas_call | solution.py:213
  42.8 3.0 %collective-permute-start.13 = (bf16[128,512]{1,0:T(8,128)(2,1)}, bf16[128,512]{1,0:T(8,128)(2,1)S(1)}, u32[]{:S(2)}, u32[]{:S(2)}) collective-permute-start(bf16[128,512]{1,0:T(8,128)(2,1)} %project_kv.3.refs_12_), channel_id=1, source_target_pairs={{0,16},{4,20},{8,24},{12,28},{16,0},{20,4},{24,8},{28,12},{1,17},{... | collective-permute-start | bytes 393224 | tf_op jit(solution)/shard_map/ppermute | solution.py:421
  45.8 1.3 %collective-permute-start.15 = (bf16[128,512]{1,0:T(8,128)(2,1)}, bf16[128,512]{1,0:T(8,128)(2,1)S(1)}, u32[]{:S(2)}, u32[]{:S(2)}) collective-permute-start(bf16[128,512]{1,0:T(8,128)(2,1)} %project_kv.3.refs_12_), channel_id=1, source_target_pairs={{0,24},{4,28},{8,16},{12,20},{16,8},{20,12},{24,0},{28,4},{1,25},{... | collective-permute-start | bytes 393224 | tf_op jit(solution)/shard_map/ppermute | solution.py:421
  47.5 1.7 %collective-permute-start.10 = (bf16[128,512]{1,0:T(8,128)(2,1)}, bf16[128,512]{1,0:T(8,128)(2,1)S(1)}, u32[]{:S(2)}, u32[]{:S(2)}) collective-permute-start(bf16[128,512]{1,0:T(8,128)(2,1)} %project_kv.3.refs_12_), channel_id=1, source_target_pairs={{0,4},{4,0},{8,12},{12,8},{16,20},{20,16},{24,28},{28,24},{1,5},{5... | collective-permute-start | bytes 393224 | tf_op jit(solution)/shard_map/ppermute | solution.py:421
  49.6 5.2 %collective-permute-done.13.refs_16_ = bf16[128,512]{1,0:T(8,128)(2,1)S(1)} collective-permute-done((bf16[128,512]{1,0:T(8,128)(2,1)}, bf16[128,512]{1,0:T(8,128)(2,1)S(1)}, u32[]{:S(2)}, u32[]{:S(2)}) %collective-permute-start.13) | collective-permute-done | bytes 131104 | tf_op jit(solution)/shard_map/ppermute | solution.py:421
  55.3 1.5 %collective-permute-start.16 = (bf16[128,512]{1,0:T(8,128)(2,1)S(1)}, bf16[128,512]{1,0:T(8,128)(2,1)S(1)}, u32[]{:S(2)}, u32[]{:S(2)}) collective-permute-start(bf16[128,512]{1,0:T(8,128)(2,1)S(1)} %collective-permute-done.15.refs_18_), channel_id=1, source_target_pairs={{0,4},{4,0},{8,12},{12,8},{16,20},{20,16},{24,28},{28,24},{1,5},{5... | collective-permute-start | bytes 393224 | tf_op jit(solution)/shard_map/ppermute | solution.py:421
  56.8 7.6 %project_q.3.refs_3_ = bf16[128,1024]{1,0:T(8,128)(2,1)} custom-call(s32[16]{0:T(128)} %refs_0_.11, f32[1,128]{1,0:T(1,128)} %constant.2.clone.refs_1_, bf16[64,4096]{1,0:T(8,128)(2,1)} %copy-done.1, bf16[64,4096]{1,0:T(8,128)(2,1)} %copy-done.2, bf16[4096,1024]{1,0:T(8,128)(2,1)} %refs_4_.7), custom_call_target="tpu_custom_call" | custom-call | flops 1073741824 | bytes 8388608 | tf_op jit(solution)/shard_map/project_q/pallas_call | solution.py:261
  65.2 9.4 %attention_far.1 = (bf16[64,4096]{1,0:T(8,128)(2,1)}, bf16[64,4096]{1,0:T(8,128)(2,1)}) custom-call(s32[16]{0:T(128)} %refs_0_.11, s32[2048]{0:T(1024)} %refs_1_.7, s32[16,128]{1,0:T(8,128)} %bitcast.1, bf16[128,1024]{1,0:T(8,128)(2,1)} %project_q.3.refs_3_, bf16[128,512]{1,0:T(8,128)(2,1)} %project_kv.2.refs_4_, bf16[128,512]{1,0:T(8,128)(2,1)} %copy-done.5, ...), custom_call_target="tpu_custom_call" | custom-call | flops 2147483648 | bytes 8388608 | tf_op jit(solution)/shard_map/attention_far/pallas_call | solution.py:393
  74.7 7.7 %project_q.2.refs_3_ = bf16[128,1024]{1,0:T(8,128)(2,1)} custom-call(s32[16]{0:T(128)} %refs_0_.11, f32[1,128]{1,0:T(1,128)} %constant.2.clone.refs_1_, bf16[64,4096]{1,0:T(8,128)(2,1)} %refs_2_.3, bf16[64,4096]{1,0:T(8,128)(2,1)} %copy-done, bf16[4096,1024]{1,0:T(8,128)(2,1)} %refs_4_.7), custom_call_target="tpu_custom_call" | custom-call | flops 1073741824 | bytes 8388608 | tf_op jit(solution)/shard_map/project_q/pallas_call | solution.py:261
  82.4 10.2 %attention_near.1 = (bf16[64,4096]{1,0:T(8,128)(2,1)}, bf16[64,4096]{1,0:T(8,128)(2,1)}) custom-call(s32[16]{0:T(128)} %refs_0_.11, s32[2048]{0:T(1024)} %refs_1_.7, s32[16,128]{1,0:T(8,128)} %bitcast.2, bf16[128,1024]{1,0:T(8,128)(2,1)} %project_q.2.refs_3_, bf16[128,512]{1,0:T(8,128)(2,1)} %project_kv.2.refs_4_, bf16[128,512]{1,0:T(8,128)(2,1)} %copy-done.5, ...), custom_call_target="tpu_custom_call" | custom-call | flops 2147483648 | bytes 8388608 | tf_op jit(solution)/shard_map/attention_near/pallas_call | solution.py:393
  93.2 1.6 %collective-permute-start.19 = (bf16[64,4096]{1,0:T(8,128)(2,1)S(1)}, bf16[64,4096]{1,0:T(8,128)(2,1)S(1)}, u32[]{:S(2)}, u32[]{:S(2)}) collective-permute-start(bf16[64,4096]{1,0:T(8,128)(2,1)S(1)} %add_convert_fusion.1), channel_id=1, source_target_pairs={{0,2},{1,3},{2,0},{3,1},{4,6},{5,7},{6,4},{7,5},{8,10},{9,11},{10,... | collective-permute-start | bytes 1572872 | tf_op jit(solution)/shard_map/ppermute | solution.py:421
  94.8 12.4 %collective-permute-done.19 = bf16[64,4096]{1,0:T(8,128)(2,1)S(1)} collective-permute-done((bf16[64,4096]{1,0:T(8,128)(2,1)S(1)}, bf16[64,4096]{1,0:T(8,128)(2,1)S(1)}, u32[]{:S(2)}, u32[]{:S(2)}) %collective-permute-start.19) | collective-permute-done | bytes 524320 | tf_op jit(solution)/shard_map/ppermute | solution.py:421
  107.2 2.0 %add_convert_fusion = bf16[64,4096]{1,0:T(8,128)(2,1)} fusion(bf16[64,4096]{1,0:T(8,128)(2,1)S(1)} %collective-permute-done.19, bf16[64,4096]{1,0:T(8,128)(2,1)S(1)} %collective-permute-done.17, bf16[64,4096]{1,0:T(8,128)(2,1)} %get-tuple-element.9), kind=kLoop, calls=%fused_computation | loop fusion | flops 1572864 | bytes 2097152 | tf_op jit(solution)/shard_map/convert_element_type | solution.py:467
  (60 shorter events, 3.7 us)
Async XLA Ops:
  0.0 15.1 %collective-permute-start.8 = (bf16[64,4096]{1,0:T(8,128)(2,1)}, bf16[64,4096]{1,0:T(8,128)(2,1)S(1)}, u32[]{:S(2)}, u32[]{:S(2)}) collective-permute-start(bf16[64,4096]{1,0:T(8,128)(2,1)} %refs_2_.3), channel_id=1, source_target_pairs={{0,2},{1,3},{2,0},{3,1},{4,6},{5,7},{6,4},{7,5},{8,10},{9,11},{10,... | collective-permute-start | bytes 1572872 | tf_op jit(solution)/shard_map/ppermute | solution.py:421
  3.0 12.1 %collective-permute-start = (bf16[64,4096]{1,0:T(8,128)(2,1)}, bf16[64,4096]{1,0:T(8,128)(2,1)S(1)}, u32[]{:S(2)}, u32[]{:S(2)}) collective-permute-start(bf16[64,4096]{1,0:T(8,128)(2,1)} %refs_2_.3), channel_id=1, source_target_pairs={{0,1},{1,0},{2,3},{3,2},{4,5},{5,4},{6,7},{7,6},{8,9},{9,8},{10,11... | collective-permute-start | bytes 1572872 | tf_op jit(solution)/shard_map/ppermute | solution.py:421
  15.1 22.1 %copy-start.1 = (bf16[64,4096]{1,0:T(8,128)(2,1)}, bf16[64,4096]{1,0:T(8,128)(2,1)S(1)}, u32[]{:S(2)}) copy-start(bf16[64,4096]{1,0:T(8,128)(2,1)S(1)} %collective-permute-done.8.refs_2_) | copy-start | bytes 1572868
  15.1 22.1 %collective-permute-start.9 = (bf16[64,4096]{1,0:T(8,128)(2,1)S(1)}, bf16[64,4096]{1,0:T(8,128)(2,1)S(1)}, u32[]{:S(2)}, u32[]{:S(2)}) collective-permute-start(bf16[64,4096]{1,0:T(8,128)(2,1)S(1)} %collective-permute-done.8.refs_2_), channel_id=1, source_target_pairs={{0,1},{1,0},{2,3},{3,2},{4,5},{5,4},{6,7},{7,6},{8,9},{9,8},{10,11... | collective-permute-start | bytes 1572872 | tf_op jit(solution)/shard_map/ppermute | solution.py:421
  20.7 8.5 %collective-permute-start.2 = (bf16[128,512]{1,0:T(8,128)(2,1)}, bf16[128,512]{1,0:T(8,128)(2,1)S(1)}, u32[]{:S(2)}, u32[]{:S(2)}) collective-permute-start(bf16[128,512]{1,0:T(8,128)(2,1)} %project_kv.2.refs_4_), channel_id=1, source_target_pairs={{0,8},{4,12},{8,0},{12,4},{16,24},{20,28},{24,16},{28,20},{1,9},{5... | collective-permute-start | bytes 393224 | tf_op jit(solution)/shard_map/ppermute | solution.py:421
  22.5 12.9 %collective-permute-start.4 = (bf16[128,512]{1,0:T(8,128)(2,1)}, bf16[128,512]{1,0:T(8,128)(2,1)S(1)}, u32[]{:S(2)}, u32[]{:S(2)}) collective-permute-start(bf16[128,512]{1,0:T(8,128)(2,1)} %project_kv.2.refs_4_), channel_id=1, source_target_pairs={{0,16},{4,20},{8,24},{12,28},{16,0},{20,4},{24,8},{28,12},{1,17},{... | collective-permute-start | bytes 393224 | tf_op jit(solution)/shard_map/ppermute | solution.py:421
  25.1 17.7 %collective-permute-start.1 = (bf16[128,512]{1,0:T(8,128)(2,1)}, bf16[128,512]{1,0:T(8,128)(2,1)S(1)}, u32[]{:S(2)}, u32[]{:S(2)}) collective-permute-start(bf16[128,512]{1,0:T(8,128)(2,1)} %project_kv.2.refs_4_), channel_id=1, source_target_pairs={{0,4},{4,0},{8,12},{12,8},{16,20},{20,16},{24,28},{28,24},{1,5},{5... | collective-permute-start | bytes 393224 | tf_op jit(solution)/shard_map/ppermute | solution.py:421
  26.6 19.2 %collective-permute-start.6 = (bf16[128,512]{1,0:T(8,128)(2,1)}, bf16[128,512]{1,0:T(8,128)(2,1)S(1)}, u32[]{:S(2)}, u32[]{:S(2)}) collective-permute-start(bf16[128,512]{1,0:T(8,128)(2,1)} %project_kv.2.refs_4_), channel_id=1, source_target_pairs={{0,24},{4,28},{8,16},{12,20},{16,8},{20,12},{24,0},{28,4},{1,25},{... | collective-permute-start | bytes 393224 | tf_op jit(solution)/shard_map/ppermute | solution.py:421
  29.2 35.2 %copy-start.3 = (bf16[128,512]{1,0:T(8,128)(2,1)}, bf16[128,512]{1,0:T(8,128)(2,1)S(1)}, u32[]{:S(2)}) copy-start(bf16[128,512]{1,0:T(8,128)(2,1)S(1)} %collective-permute-done.2.refs_6_) | copy-start | bytes 393220
  29.2 18.0 %collective-permute-start.3 = (bf16[128,512]{1,0:T(8,128)(2,1)S(1)}, bf16[128,512]{1,0:T(8,128)(2,1)S(1)}, u32[]{:S(2)}, u32[]{:S(2)}) collective-permute-start(bf16[128,512]{1,0:T(8,128)(2,1)S(1)} %collective-permute-done.2.refs_6_), channel_id=1, source_target_pairs={{0,4},{4,0},{8,12},{12,8},{16,20},{20,16},{24,28},{28,24},{1,5},{5... | collective-permute-start | bytes 393224 | tf_op jit(solution)/shard_map/ppermute | solution.py:421
  35.5 29.0 %copy-start.4 = (bf16[128,512]{1,0:T(8,128)(2,1)}, bf16[128,512]{1,0:T(8,128)(2,1)S(1)}, u32[]{:S(2)}) copy-start(bf16[128,512]{1,0:T(8,128)(2,1)S(1)} %collective-permute-done.4.refs_8_) | copy-start | bytes 393220
  35.5 12.0 %collective-permute-start.5 = (bf16[128,512]{1,0:T(8,128)(2,1)S(1)}, bf16[128,512]{1,0:T(8,128)(2,1)S(1)}, u32[]{:S(2)}, u32[]{:S(2)}) collective-permute-start(bf16[128,512]{1,0:T(8,128)(2,1)S(1)} %collective-permute-done.4.refs_8_), channel_id=1, source_target_pairs={{0,4},{4,0},{8,12},{12,8},{16,20},{20,16},{24,28},{28,24},{1,5},{5... | collective-permute-start | bytes 393224 | tf_op jit(solution)/shard_map/ppermute | solution.py:421
  42.7 6.5 %collective-permute-start.11 = (bf16[128,512]{1,0:T(8,128)(2,1)}, bf16[128,512]{1,0:T(8,128)(2,1)S(1)}, u32[]{:S(2)}, u32[]{:S(2)}) collective-permute-start(bf16[128,512]{1,0:T(8,128)(2,1)} %project_kv.3.refs_12_), channel_id=1, source_target_pairs={{0,8},{4,12},{8,0},{12,4},{16,24},{20,28},{24,16},{28,20},{1,9},{5... | collective-permute-start | bytes 393224 | tf_op jit(solution)/shard_map/ppermute | solution.py:421
  42.8 21.7 %copy-start.5 = (bf16[128,512]{1,0:T(8,128)(2,1)}, bf16[128,512]{1,0:T(8,128)(2,1)S(1)}, u32[]{:S(2)}) copy-start(bf16[128,512]{1,0:T(8,128)(2,1)S(1)} %collective-permute-done.1.refs_5_) | copy-start | bytes 393220
  42.8 11.9 %collective-permute-start.13 = (bf16[128,512]{1,0:T(8,128)(2,1)}, bf16[128,512]{1,0:T(8,128)(2,1)S(1)}, u32[]{:S(2)}, u32[]{:S(2)}) collective-permute-start(bf16[128,512]{1,0:T(8,128)(2,1)} %project_kv.3.refs_12_), channel_id=1, source_target_pairs={{0,16},{4,20},{8,24},{12,28},{16,0},{20,4},{24,8},{28,12},{1,17},{... | collective-permute-start | bytes 393224 | tf_op jit(solution)/shard_map/ppermute | solution.py:421
  45.8 9.4 %collective-permute-start.15 = (bf16[128,512]{1,0:T(8,128)(2,1)}, bf16[128,512]{1,0:T(8,128)(2,1)S(1)}, u32[]{:S(2)}, u32[]{:S(2)}) collective-permute-start(bf16[128,512]{1,0:T(8,128)(2,1)} %project_kv.3.refs_12_), channel_id=1, source_target_pairs={{0,24},{4,28},{8,16},{12,20},{16,8},{20,12},{24,0},{28,4},{1,25},{... | collective-permute-start | bytes 393224 | tf_op jit(solution)/shard_map/ppermute | solution.py:421
  47.2 17.2 %collective-permute-start.7 = (bf16[128,512]{1,0:T(8,128)(2,1)S(1)}, bf16[128,512]{1,0:T(8,128)(2,1)S(1)}, u32[]{:S(2)}, u32[]{:S(2)}) collective-permute-start(bf16[128,512]{1,0:T(8,128)(2,1)S(1)} %collective-permute-done.6.refs_10_), channel_id=1, source_target_pairs={{0,4},{4,0},{8,12},{12,8},{16,20},{20,16},{24,28},{28,24},{1,5},{5... | collective-permute-start | bytes 393224 | tf_op jit(solution)/shard_map/ppermute | solution.py:421
  47.5 16.9 %collective-permute-start.10 = (bf16[128,512]{1,0:T(8,128)(2,1)}, bf16[128,512]{1,0:T(8,128)(2,1)S(1)}, u32[]{:S(2)}, u32[]{:S(2)}) collective-permute-start(bf16[128,512]{1,0:T(8,128)(2,1)} %project_kv.3.refs_12_), channel_id=1, source_target_pairs={{0,4},{4,0},{8,12},{12,8},{16,20},{20,16},{24,28},{28,24},{1,5},{5... | collective-permute-start | bytes 393224 | tf_op jit(solution)/shard_map/ppermute | solution.py:421
  49.2 15.2 %collective-permute-start.12 = (bf16[128,512]{1,0:T(8,128)(2,1)S(1)}, bf16[128,512]{1,0:T(8,128)(2,1)S(1)}, u32[]{:S(2)}, u32[]{:S(2)}) collective-permute-start(bf16[128,512]{1,0:T(8,128)(2,1)S(1)} %collective-permute-done.11.refs_14_), channel_id=1, source_target_pairs={{0,4},{4,0},{8,12},{12,8},{16,20},{20,16},{24,28},{28,24},{1,5},{5... | collective-permute-start | bytes 393224 | tf_op jit(solution)/shard_map/ppermute | solution.py:421
  54.8 9.7 %collective-permute-start.14 = (bf16[128,512]{1,0:T(8,128)(2,1)S(1)}, bf16[128,512]{1,0:T(8,128)(2,1)S(1)}, u32[]{:S(2)}, u32[]{:S(2)}) collective-permute-start(bf16[128,512]{1,0:T(8,128)(2,1)S(1)} %collective-permute-done.13.refs_16_), channel_id=1, source_target_pairs={{0,4},{4,0},{8,12},{12,8},{16,20},{20,16},{24,28},{28,24},{1,5},{5... | collective-permute-start | bytes 393224 | tf_op jit(solution)/shard_map/ppermute | solution.py:421
  55.3 9.1 %collective-permute-start.16 = (bf16[128,512]{1,0:T(8,128)(2,1)S(1)}, bf16[128,512]{1,0:T(8,128)(2,1)S(1)}, u32[]{:S(2)}, u32[]{:S(2)}) collective-permute-start(bf16[128,512]{1,0:T(8,128)(2,1)S(1)} %collective-permute-done.15.refs_18_), channel_id=1, source_target_pairs={{0,4},{4,0},{8,12},{12,8},{16,20},{20,16},{24,28},{28,24},{1,5},{5... | collective-permute-start | bytes 393224 | tf_op jit(solution)/shard_map/ppermute | solution.py:421
  74.6 18.5 %collective-permute-start.18 = (bf16[64,4096]{1,0:T(8,128)(2,1)}, bf16[64,4096]{1,0:T(8,128)(2,1)S(1)}, u32[]{:S(2)}, u32[]{:S(2)}) collective-permute-start(bf16[64,4096]{1,0:T(8,128)(2,1)} %get-tuple-element.12), channel_id=1, source_target_pairs={{0,1},{1,0},{2,3},{3,2},{4,5},{5,4},{6,7},{7,6},{8,9},{9,8},{10,11... | collective-permute-start | bytes 1572872 | tf_op jit(solution)/shard_map/ppermute | solution.py:421
  92.6 2.2 %collective-permute-start.17 = (bf16[64,4096]{1,0:T(8,128)(2,1)}, bf16[64,4096]{1,0:T(8,128)(2,1)S(1)}, u32[]{:S(2)}, u32[]{:S(2)}) collective-permute-start(bf16[64,4096]{1,0:T(8,128)(2,1)} %get-tuple-element.10), channel_id=1, source_target_pairs={{0,1},{1,0},{2,3},{3,2},{4,5},{5,4},{6,7},{7,6},{8,9},{9,8},{10,11... | collective-permute-start | bytes 1572872 | tf_op jit(solution)/shard_map/ppermute | solution.py:421
  93.2 14.0 %collective-permute-start.19 = (bf16[64,4096]{1,0:T(8,128)(2,1)S(1)}, bf16[64,4096]{1,0:T(8,128)(2,1)S(1)}, u32[]{:S(2)}, u32[]{:S(2)}) collective-permute-start(bf16[64,4096]{1,0:T(8,128)(2,1)S(1)} %add_convert_fusion.1), channel_id=1, source_target_pairs={{0,2},{1,3},{2,0},{3,1},{4,6},{5,7},{6,4},{7,5},{8,10},{9,11},{10,... | collective-permute-start | bytes 1572872 | tf_op jit(solution)/shard_map/ppermute | solution.py:421
  (14 other events, 110.9 us)

commit v2 on v1

--- a/solution.py
+++ b/solution.py
@@ -174,7 +174,7 @@
 
 
 def kv_kernel(
-    order_ref, freq_ref, own_ref, peer_ref, wk_ref, wv_ref, out_ref, x_ref, k_vmem, v_vmem, xs, ws, *, far
+    first_ref, second_ref, own_ref, peer_ref, wk_ref, wv_ref, out_ref, x_ref, k_vmem, v_vmem, xs, ws, *, far
 ):
     rows, depth = own_ref.shape
     width = wk_ref.shape[1]
@@ -188,7 +188,10 @@
             copy = pltpu.make_async_copy(src.at[cut], dst.at[cut], ws.at[which, at])
             copy.start()
             copies.append(copy)
-    cosine, sine = angles(order_ref[stored_block(far)], freq_ref, 2 * rows)
+    if far:
+        cosine, sine = first_ref[...], second_ref[...]
+    else:
+        cosine, sine = angles(first_ref[stored_block(far)], second_ref, 2 * rows)
     for copy in x_copies:
         copy.wait()
     keys = values = None
@@ -206,13 +209,33 @@
     out_ref[:, width:] = values.astype(BF16)
 
 
-def project_kv(order, freqs, own, peer, wk, wv, far):
+def tables_kernel(order_ref, freq_ref, cos_ref, sin_ref):
+    cos_ref[...], sin_ref[...] = angles(
+        order_ref[stored_block(True)], freq_ref, cos_ref.shape[0]
+    )
+
+
+def rotary_tables(order, freqs, block):
+    shape = jax.ShapeDtypeStruct((block, HEAD_SIZE), F32)
+    return pl.pallas_call(
+        tables_kernel,
+        in_specs=[SMEM, VMEM],
+        out_specs=[VMEM] * 2,
+        out_shape=[shape] * 2,
+        cost_estimate=pl.CostEstimate(
+            flops=64 * block * HEAD_SIZE, bytes_accessed=8 * block * HEAD_SIZE, transcendentals=0
+        ),
+        name="rotary_tables",
+    )(order, freqs)
+
+
+def project_kv(first, second, own, peer, wk, wv, far):
     rows, depth = own.shape
     width = wk.shape[1]
     parts = 4
     return pl.pallas_call(
         lambda *refs: kv_kernel(*refs, far=far),
-        in_specs=[SMEM, VMEM, ANY, ANY, ANY, ANY],
+        in_specs=[VMEM if far else SMEM, VMEM, ANY, ANY, ANY, ANY],
         out_specs=VMEM,
         out_shape=jax.ShapeDtypeStruct((2 * rows, 2 * width), BF16),
         scratch_shapes=[
@@ -226,13 +249,17 @@
             flops=8 * rows * depth * width, bytes_accessed=4 * depth * width, transcendentals=0
         ),
         name="project_kv",
-    )(order, freqs, own, peer, wk, wv)
-
-
-def q_kernel(order_ref, freq_ref, own_ref, peer_ref, w_ref, out_ref, x_ref, w_vmem, xs, ws, *, far):
-    rows = own_ref.shape[0]
+    )(first, second, own, peer, wk, wv)
+
+
+def q_kernel(
+    order_ref, freq_ref, cos_ref, sin_ref, a_ref, b_ref, c_ref, d_ref, w_ref, out_ref,
+    x_ref, w_vmem, xs, ws,
+):
+    rows = a_ref.shape[0]
     tiles, _, tile = w_vmem.shape
-    x_copies = start_rows(own_ref, peer_ref, x_ref, 0, xs)
+    x_copies = start_rows(a_ref, b_ref, x_ref, 0, xs.at[0])
+    x_copies += start_rows(c_ref, d_ref, x_ref, 2 * rows, xs.at[1])
     copies = []
     for at in range(tiles):
         copy = pltpu.make_async_copy(
@@ -240,7 +267,9 @@
         )
         copy.start()
         copies.append(copy)
-    cosine, sine = angles(order_ref[stored_block(far)], freq_ref, 2 * rows)
+    cosine, sine = angles(order_ref[stored_block(False)], freq_ref, 2 * rows)
+    cosine = jnp.concatenate([cosine, cos_ref[...]], axis=0)
+    sine = jnp.concatenate([sine, sin_ref[...]], axis=0)
     for copy in x_copies:
         copy.wait()
     for at in range(tiles):
@@ -253,27 +282,27 @@
             ).astype(BF16)
 
 
-def project_q(order, freqs, own, peer, weight, far):
-    rows, depth = own.shape
+def project_q(order, freqs, tables, pieces, weight):
+    rows, depth = pieces[0].shape
     width = weight.shape[1]
     tile = 2 * HEAD_SIZE
     tiles = width // tile
     return pl.pallas_call(
-        lambda *refs: q_kernel(*refs, far=far),
-        in_specs=[SMEM, VMEM] + [ANY] * 3,
+        q_kernel,
+        in_specs=[SMEM, VMEM, VMEM, VMEM] + [ANY] * 5,
         out_specs=VMEM,
-        out_shape=jax.ShapeDtypeStruct((2 * rows, width), BF16),
+        out_shape=jax.ShapeDtypeStruct((4 * rows, width), BF16),
         scratch_shapes=[
-            pltpu.VMEM((2 * rows, depth), BF16),
+            pltpu.VMEM((4 * rows, depth), BF16),
             pltpu.VMEM((tiles, depth, tile), BF16),
-            pltpu.SemaphoreType.DMA((2,)),
+            pltpu.SemaphoreType.DMA((2, 2)),
             pltpu.SemaphoreType.DMA((tiles,)),
         ],
         cost_estimate=pl.CostEstimate(
-            flops=4 * rows * depth * width, bytes_accessed=2 * depth * width, transcendentals=0
+            flops=8 * rows * depth * width, bytes_accessed=2 * depth * width, transcendentals=0
         ),
         name="project_q",
-    )(order, freqs, own, peer, weight)
+    )(order, freqs, *tables, *pieces, weight)
 
 
 def attention_kernel(
@@ -319,7 +348,7 @@
     )
     for head in range(kv_heads * group):
         qs_ref[head * block : (head + 1) * block, :] = q_ref[
-            :, head * HEAD_SIZE : (head + 1) * HEAD_SIZE
+            block * far : block * (far + 1), head * HEAD_SIZE : (head + 1) * HEAD_SIZE
         ]
     m_ref[...] = jnp.full_like(m_ref, NEGATIVE_FILLER)
     l_ref[...] = jnp.zeros_like(l_ref)
@@ -424,13 +453,16 @@
 def gather_seq(piece, shards, lanes):
     found = {0: piece}
     far = range(lanes, shards, lanes)
+    for near in range(1, lanes):
+        found[near] = swap(piece, "seq", shards, near)
     for step in sorted(far, reverse=True):
         found[step] = swap(piece, "seq", shards, step)
-    for near in range(1, lanes):
-        found[near] = swap(piece, "seq", shards, near)
     for step in far:
         for near in range(1, lanes):
-            found[step + near] = swap(found[step], "seq", shards, near)
+            if step == lanes:
+                found[step + near] = swap(found[near], "seq", shards, step)
+            else:
+                found[step + near] = swap(found[step], "seq", shards, near)
     return [found[step] for step in range(shards)]
 
 
@@ -445,24 +477,26 @@
         freqs = frequencies()
         across = swap(hidden, "head", 4, 2)
         beside = swap(hidden, "head", 4, 1)
+        tables = rotary_tables(order, freqs, seg_rows.shape[1])
         early = project_kv(order, freqs, hidden, beside, key_weight, value_weight, False)
         early_all = gather_seq(early, shards, lanes)
         across_beside = swap(across, "head", 4, 1)
-        late = project_kv(order, freqs, across, across_beside, key_weight, value_weight, True)
+        late = project_kv(*tables, across, across_beside, key_weight, value_weight, True)
         late_all = gather_seq(late, shards, lanes)
-        near_queries = project_q(order, freqs, hidden, beside, w_query, False)
-        far_queries = project_q(order, freqs, across, across_beside, w_query, True)
+        queries = project_q(
+            order, freqs, tables, (hidden, beside, across, across_beside), w_query
+        )
 
         def attend_rows(q, far):
             return attention_out(
                 order, segment_ids, seg_rows, q, early_all + late_all, w_out, kv_heads, group, far
             )
 
-        far_own, far_peer = attend_rows(far_queries, True)
+        far_own, far_peer = attend_rows(queries, True)
         far_in = swap(far_peer, "head", 4, 1)
         crossing = (far_own.astype(F32) + far_in.astype(F32)).astype(BF16)
         crossed = swap(crossing, "head", 4, 2)
-        near_own, near_peer = attend_rows(near_queries, False)
+        near_own, near_peer = attend_rows(queries, False)
         near_in = swap(near_peer, "head", 4, 1)
         return (near_own.astype(F32) + near_in.astype(F32) + crossed.astype(F32)).astype(BF16)
 

time: 110 us -> 103 us (0.936)
  waiting for transfers between devices: 36.9 us -> 33.4 us
  Pallas kernels: 44.3 us -> 41.6 us
    ppermute x20, waiting for transfers between devices: 36.9 us -> 33.4 us  [swap(): return lax.ppermute(values, axis, [(at, at ^ mask) for at in range(count)])]
    pallas_call x4, Pallas kernels: 24.7 us -> 21.8 us  [the longest x1 10.4 us: project_q(): pl.pallas_call(q_kernel, in_specs=[SMEM, VMEM, VMEM, VMEM] + [ANY] * 5, o...]
  transfers between devices with their start and end apart: 20 -> 20, of which waited for: 5 -> 4; matrix products, arithmetic and copies ran while one was open for 0% -> 0% of each run, Pallas kernels for 32% -> 31%
where the time goes in v2:
time: 103 us
  Pallas kernels  41.6 us (40%)
  waiting for transfers between devices  33.4 us (32%)
  starting transfers between devices  23.3 us (23%)
  local copies, waits for them, and re-layouts  2.33 us (2%)
  other arithmetic  2.15 us (2%)
    ppermute x20, waiting for transfers between devices, swap(): return lax.ppermute(values, axis, [(at, at ^ mask) for at in range(count)])  33.4 us
    ppermute x20, starting transfers between devices, swap(): return lax.ppermute(values, axis, [(at, at ^ mask) for at in range(count)])  23.3 us
    pallas_call x2, Pallas kernels, attention_out(): pl.pallas_call(kernel, in_specs=[SMEM, SMEM, VMEM, VMEM] + [ANY] * (count...  19.9 us
    pallas_call x1, Pallas kernels, project_q(): pl.pallas_call(q_kernel, in_specs=[SMEM, VMEM, VMEM, VMEM] + [ANY] * 5, o...  10.4 us
    pallas_call x2, Pallas kernels, project_kv(): pl.pallas_call(lambda *refs: kv_kernel(*refs, far=far), in_specs=[VMEM if...  9.78 us
    unnamed x36, local copies, waits for them, and re-layouts  2.33 us
  transfers between devices with their start and end apart: 20, of which 4 were waited for; matrix products, arithmetic and copies ran while one was open for 0% of the time, Pallas kernels for 31%

profile of v2, /device:TPU:0, one launch (start us, length us, event | category | flops | bytes accessed | tf_op | source)
XLA Modules:
  0.0 103.0 jit_solution(17595644917848270627)
XLA Ops:
  0.0 3.0 %collective-permute-start.1 = (bf16[64,4096]{1,0:T(8,128)(2,1)}, bf16[64,4096]{1,0:T(8,128)(2,1)S(1)}, u32[]{:S(2)}, u32[]{:S(2)}) collective-permute-start(bf16[64,4096]{1,0:T(8,128)(2,1)} %refs_2_.1), channel_id=1, source_target_pairs={{0,2},{1,3},{2,0},{3,1},{4,6},{5,7},{6,4},{7,5},{8,10},{9,11},{10,... | collective-permute-start | bytes 1572872 | tf_op jit(solution)/shard_map/ppermute | solution.py:450
  3.0 12.1 %collective-permute-done.1.c_ref.refs_2_ = bf16[64,4096]{1,0:T(8,128)(2,1)S(1)} collective-permute-done((bf16[64,4096]{1,0:T(8,128)(2,1)}, bf16[64,4096]{1,0:T(8,128)(2,1)S(1)}, u32[]{:S(2)}, u32[]{:S(2)}) %collective-permute-start.1) | collective-permute-done | bytes 524320 | tf_op jit(solution)/shard_map/ppermute | solution.py:450
  15.2 0.8 copy-done
  16.0 4.7 %project_kv.2.refs_4_ = bf16[128,512]{1,0:T(8,128)(2,1)} custom-call(s32[16]{0:T(128)} %refs_0_.5, f32[1,128]{1,0:T(1,128)} %constant.2.clone.freq_ref.refs_1_, bf16[64,4096]{1,0:T(8,128)(2,1)} %refs_2_.1, bf16[64,4096]{1,0:T(8,128)(2,1)} %copy-done, bf16[4096,256]{1,0:T(8,128)(2,1)} %refs_4_.3, bf16[4096,256]{1,0:T(8,128)(2,1)} %refs_5_.3), custom_call_target="tpu_custom_call" | custom-call | flops 536870912 | bytes 4194304 | tf_op jit(solution)/shard_map/project_kv/pallas_call | solution.py:236
  20.7 1.8 %collective-permute-start.3 = (bf16[128,512]{1,0:T(8,128)(2,1)}, bf16[128,512]{1,0:T(8,128)(2,1)S(1)}, u32[]{:S(2)}, u32[]{:S(2)}) collective-permute-start(bf16[128,512]{1,0:T(8,128)(2,1)} %project_kv.2.refs_4_), channel_id=1, source_target_pairs={{0,4},{4,0},{8,12},{12,8},{16,20},{20,16},{24,28},{28,24},{1,5},{5... | collective-permute-start | bytes 393224 | tf_op jit(solution)/shard_map/ppermute | solution.py:450
  22.5 2.6 %collective-permute-start.6 = (bf16[128,512]{1,0:T(8,128)(2,1)}, bf16[128,512]{1,0:T(8,128)(2,1)S(1)}, u32[]{:S(2)}, u32[]{:S(2)}) collective-permute-start(bf16[128,512]{1,0:T(8,128)(2,1)} %project_kv.2.refs_4_), channel_id=1, source_target_pairs={{0,16},{4,20},{8,24},{12,28},{16,0},{20,4},{24,8},{28,12},{1,17},{... | collective-permute-start | bytes 393224 | tf_op jit(solution)/shard_map/ppermute | solution.py:450
  25.0 1.6 %collective-permute-start.4 = (bf16[128,512]{1,0:T(8,128)(2,1)}, bf16[128,512]{1,0:T(8,128)(2,1)S(1)}, u32[]{:S(2)}, u32[]{:S(2)}) collective-permute-start(bf16[128,512]{1,0:T(8,128)(2,1)} %project_kv.2.refs_4_), channel_id=1, source_target_pairs={{0,8},{4,12},{8,0},{12,4},{16,24},{20,28},{24,16},{28,20},{1,9},{5... | collective-permute-start | bytes 393224 | tf_op jit(solution)/shard_map/ppermute | solution.py:450
  26.8 1.6 %rotary_tables.1 = (f32[128,128]{1,0:T(8,128)}, f32[128,128]{1,0:T(8,128)}) custom-call(s32[16]{0:T(128)} %refs_0_.5, f32[1,128]{1,0:T(1,128)} %constant.2.clone.freq_ref.refs_1_), custom_call_target="tpu_custom_call" | custom-call | flops 1048576 | bytes 131072 | tf_op jit(solution)/shard_map/rotary_tables/pallas_call | solution.py:220
  28.4 0.7 collective-permute-start.5
  29.2 4.0 %collective-permute-done.6.refs_8_ = bf16[128,512]{1,0:T(8,128)(2,1)S(1)} collective-permute-done((bf16[128,512]{1,0:T(8,128)(2,1)}, bf16[128,512]{1,0:T(8,128)(2,1)S(1)}, u32[]{:S(2)}, u32[]{:S(2)}) %collective-permute-start.6) | collective-permute-done | bytes 131104 | tf_op jit(solution)/shard_map/ppermute | solution.py:450
  33.3 0.8 copy-done.2
  34.1 5.1 %project_kv.3.refs_12_ = bf16[128,512]{1,0:T(8,128)(2,1)} custom-call(f32[128,128]{1,0:T(8,128)} %get-tuple-element.11.cos_ref.refs_0_, f32[128,128]{1,0:T(8,128)} %get-tuple-element.12.sin_ref.refs_1_, bf16[64,4096]{1,0:T(8,128)(2,1)} %copy-done.1, bf16[64,4096]{1,0:T(8,128)(2,1)} %copy-done.2, bf16[4096,256]{1,0:T(8,128)(2,1)} %refs_4_.3, ...), custom_call_target="tpu_custom_call" | custom-call | flops 536870912 | bytes 4194304 | tf_op jit(solution)/shard_map/project_kv/pallas_call | solution.py:236
  39.2 2.0 %collective-permute-start.10 = (bf16[128,512]{1,0:T(8,128)(2,1)}, bf16[128,512]{1,0:T(8,128)(2,1)S(1)}, u32[]{:S(2)}, u32[]{:S(2)}) collective-permute-start(bf16[128,512]{1,0:T(8,128)(2,1)} %project_kv.3.refs_12_), channel_id=1, source_target_pairs={{0,4},{4,0},{8,12},{12,8},{16,20},{20,16},{24,28},{28,24},{1,5},{5... | collective-permute-start | bytes 393224 | tf_op jit(solution)/shard_map/ppermute | solution.py:450
  41.2 4.6 %collective-permute-start.15 = (bf16[128,512]{1,0:T(8,128)(2,1)}, bf16[128,512]{1,0:T(8,128)(2,1)S(1)}, u32[]{:S(2)}, u32[]{:S(2)}) collective-permute-start(bf16[128,512]{1,0:T(8,128)(2,1)} %project_kv.3.refs_12_), channel_id=1, source_target_pairs={{0,24},{4,28},{8,16},{12,20},{16,8},{20,12},{24,0},{28,4},{1,25},{... | collective-permute-start | bytes 393224 | tf_op jit(solution)/shard_map/ppermute | solution.py:450
  46.3 0.6 collective-permute-start.11
  46.9 1.5 %collective-permute-start.12 = (bf16[128,512]{1,0:T(8,128)(2,1)S(1)}, bf16[128,512]{1,0:T(8,128)(2,1)S(1)}, u32[]{:S(2)}, u32[]{:S(2)}) collective-permute-start(bf16[128,512]{1,0:T(8,128)(2,1)S(1)} %collective-permute-done.10.refs_13_), channel_id=1, source_target_pairs={{0,8},{4,12},{8,0},{12,4},{16,24},{20,28},{24,16},{28,20},{1,9},{5... | collective-permute-start | bytes 393224 | tf_op jit(solution)/shard_map/ppermute | solution.py:450
  48.3 4.8 %collective-permute-done.13.refs_16_ = bf16[128,512]{1,0:T(8,128)(2,1)S(1)} collective-permute-done((bf16[128,512]{1,0:T(8,128)(2,1)}, bf16[128,512]{1,0:T(8,128)(2,1)S(1)}, u32[]{:S(2)}, u32[]{:S(2)}) %collective-permute-start.13) | collective-permute-done | bytes 131104 | tf_op jit(solution)/shard_map/ppermute | solution.py:450
  53.6 1.5 %collective-permute-start.16 = (bf16[128,512]{1,0:T(8,128)(2,1)S(1)}, bf16[128,512]{1,0:T(8,128)(2,1)S(1)}, u32[]{:S(2)}, u32[]{:S(2)}) collective-permute-start(bf16[128,512]{1,0:T(8,128)(2,1)S(1)} %collective-permute-done.15.refs_18_), channel_id=1, source_target_pairs={{0,4},{4,0},{8,12},{12,8},{16,20},{20,16},{24,28},{28,24},{1,5},{5... | collective-permute-start | bytes 393224 | tf_op jit(solution)/shard_map/ppermute | solution.py:450
  55.2 10.4 %project_q.1.refs_3_ = bf16[256,1024]{1,0:T(8,128)(2,1)} custom-call(s32[16]{0:T(128)} %refs_0_.5, f32[1,128]{1,0:T(1,128)} %constant.2.clone.freq_ref.refs_1_, f32[128,128]{1,0:T(8,128)} %get-tuple-element.11.cos_ref.refs_0_, f32[128,128]{1,0:T(8,128)} %get-tuple-element.12.sin_ref.refs_1_, bf16[64,4096]{1,0:T(8,128)(2,1)} %refs_2_.1, ...), custom_call_target="tpu_custom_call" | custom-call | flops 2147483648 | bytes 8388608 | tf_op jit(solution)/shard_map/project_q/pallas_call | solution.py:290
  66.4 9.5 %attention_far.1 = (bf16[64,4096]{1,0:T(8,128)(2,1)}, bf16[64,4096]{1,0:T(8,128)(2,1)}) custom-call(s32[16]{0:T(128)} %refs_0_.5, s32[2048]{0:T(1024)} %refs_1_.4, s32[16,128]{1,0:T(8,128)} %bitcast.1, bf16[256,1024]{1,0:T(8,128)(2,1)} %project_q.1.refs_3_, bf16[128,512]{1,0:T(8,128)(2,1)} %project_kv.2.refs_4_, bf16[128,512]{1,0:T(8,128)(2,1)} %copy-done.3, ...), custom_call_target="tpu_custom_call" | custom-call | flops 2147483648 | bytes 8388608 | tf_op jit(solution)/shard_map/attention_far/pallas_call | solution.py:422
  76.0 10.4 %attention_near.1 = (bf16[64,4096]{1,0:T(8,128)(2,1)}, bf16[64,4096]{1,0:T(8,128)(2,1)}) custom-call(s32[16]{0:T(128)} %refs_0_.5, s32[2048]{0:T(1024)} %refs_1_.4, s32[16,128]{1,0:T(8,128)} %bitcast.2, bf16[256,1024]{1,0:T(8,128)(2,1)} %project_q.1.refs_3_, bf16[128,512]{1,0:T(8,128)(2,1)} %project_kv.2.refs_4_, bf16[128,512]{1,0:T(8,128)(2,1)} %copy-done.3, ...), custom_call_target="tpu_custom_call" | custom-call | flops 2147483648 | bytes 8388608 | tf_op jit(solution)/shard_map/attention_near/pallas_call | solution.py:422
  87.0 1.6 %collective-permute-start.19 = (bf16[64,4096]{1,0:T(8,128)(2,1)S(1)}, bf16[64,4096]{1,0:T(8,128)(2,1)S(1)}, u32[]{:S(2)}, u32[]{:S(2)}) collective-permute-start(bf16[64,4096]{1,0:T(8,128)(2,1)S(1)} %add_convert_fusion.1), channel_id=1, source_target_pairs={{0,2},{1,3},{2,0},{3,1},{4,6},{5,7},{6,4},{7,5},{8,10},{9,11},{10,... | collective-permute-start | bytes 1572872 | tf_op jit(solution)/shard_map/ppermute | solution.py:450
  88.6 12.4 %collective-permute-done.19 = bf16[64,4096]{1,0:T(8,128)(2,1)S(1)} collective-permute-done((bf16[64,4096]{1,0:T(8,128)(2,1)S(1)}, bf16[64,4096]{1,0:T(8,128)(2,1)S(1)}, u32[]{:S(2)}, u32[]{:S(2)}) %collective-permute-start.19) | collective-permute-done | bytes 524320 | tf_op jit(solution)/shard_map/ppermute | solution.py:450
  101.0 2.0 %add_convert_fusion = bf16[64,4096]{1,0:T(8,128)(2,1)} fusion(bf16[64,4096]{1,0:T(8,128)(2,1)S(1)} %collective-permute-done.19, bf16[64,4096]{1,0:T(8,128)(2,1)S(1)} %collective-permute-done.17, bf16[64,4096]{1,0:T(8,128)(2,1)} %get-tuple-element.13), kind=kLoop, calls=%fused_computation | loop fusion | flops 1572864 | bytes 2097152 | tf_op jit(solution)/shard_map/convert_element_type | solution.py:501
  (60 shorter events, 2.8 us)
Async XLA Ops:
  0.0 15.1 %collective-permute-start.1 = (bf16[64,4096]{1,0:T(8,128)(2,1)}, bf16[64,4096]{1,0:T(8,128)(2,1)S(1)}, u32[]{:S(2)}, u32[]{:S(2)}) collective-permute-start(bf16[64,4096]{1,0:T(8,128)(2,1)} %refs_2_.1), channel_id=1, source_target_pairs={{0,2},{1,3},{2,0},{3,1},{4,6},{5,7},{6,4},{7,5},{8,10},{9,11},{10,... | collective-permute-start | bytes 1572872 | tf_op jit(solution)/shard_map/ppermute | solution.py:450
  3.0 12.1 %collective-permute-start = (bf16[64,4096]{1,0:T(8,128)(2,1)}, bf16[64,4096]{1,0:T(8,128)(2,1)S(1)}, u32[]{:S(2)}, u32[]{:S(2)}) collective-permute-start(bf16[64,4096]{1,0:T(8,128)(2,1)} %refs_2_.1), channel_id=1, source_target_pairs={{0,1},{1,0},{2,3},{3,2},{4,5},{5,4},{6,7},{7,6},{8,9},{9,8},{10,11... | collective-permute-start | bytes 1572872 | tf_op jit(solution)/shard_map/ppermute | solution.py:450
  15.1 18.2 %collective-permute-start.2 = (bf16[64,4096]{1,0:T(8,128)(2,1)S(1)}, bf16[64,4096]{1,0:T(8,128)(2,1)S(1)}, u32[]{:S(2)}, u32[]{:S(2)}) collective-permute-start(bf16[64,4096]{1,0:T(8,128)(2,1)S(1)} %collective-permute-done.1.c_ref.refs_2_), channel_id=1, source_target_pairs={{0,1},{1,0},{2,3},{3,2},{4,5},{5,4},{6,7},{7,6},{8,9},{9,8},{10,11... | collective-permute-start | bytes 1572872 | tf_op jit(solution)/shard_map/ppermute | solution.py:450
  20.7 7.8 %collective-permute-start.3 = (bf16[128,512]{1,0:T(8,128)(2,1)}, bf16[128,512]{1,0:T(8,128)(2,1)S(1)}, u32[]{:S(2)}, u32[]{:S(2)}) collective-permute-start(bf16[128,512]{1,0:T(8,128)(2,1)} %project_kv.2.refs_4_), channel_id=1, source_target_pairs={{0,4},{4,0},{8,12},{12,8},{16,20},{20,16},{24,28},{28,24},{1,5},{5... | collective-permute-start | bytes 393224 | tf_op jit(solution)/shard_map/ppermute | solution.py:450
  22.5 10.7 %collective-permute-start.6 = (bf16[128,512]{1,0:T(8,128)(2,1)}, bf16[128,512]{1,0:T(8,128)(2,1)S(1)}, u32[]{:S(2)}, u32[]{:S(2)}) collective-permute-start(bf16[128,512]{1,0:T(8,128)(2,1)} %project_kv.2.refs_4_), channel_id=1, source_target_pairs={{0,16},{4,20},{8,24},{12,28},{16,0},{20,4},{24,8},{28,12},{1,17},{... | collective-permute-start | bytes 393224 | tf_op jit(solution)/shard_map/ppermute | solution.py:450
  25.0 16.1 %collective-permute-start.4 = (bf16[128,512]{1,0:T(8,128)(2,1)}, bf16[128,512]{1,0:T(8,128)(2,1)S(1)}, u32[]{:S(2)}, u32[]{:S(2)}) collective-permute-start(bf16[128,512]{1,0:T(8,128)(2,1)} %project_kv.2.refs_4_), channel_id=1, source_target_pairs={{0,8},{4,12},{8,0},{12,4},{16,24},{20,28},{24,16},{28,20},{1,9},{5... | collective-permute-start | bytes 393224 | tf_op jit(solution)/shard_map/ppermute | solution.py:450
  26.6 14.6 %collective-permute-start.8 = (bf16[128,512]{1,0:T(8,128)(2,1)}, bf16[128,512]{1,0:T(8,128)(2,1)S(1)}, u32[]{:S(2)}, u32[]{:S(2)}) collective-permute-start(bf16[128,512]{1,0:T(8,128)(2,1)} %project_kv.2.refs_4_), channel_id=1, source_target_pairs={{0,24},{4,28},{8,16},{12,20},{16,8},{20,12},{24,0},{28,4},{1,25},{... | collective-permute-start | bytes 393224 | tf_op jit(solution)/shard_map/ppermute | solution.py:450
  28.4 37.2 %copy-start.3 = (bf16[128,512]{1,0:T(8,128)(2,1)}, bf16[128,512]{1,0:T(8,128)(2,1)S(1)}, u32[]{:S(2)}) copy-start(bf16[128,512]{1,0:T(8,128)(2,1)S(1)} %collective-permute-done.3.refs_5_) | copy-start | bytes 393220
  28.4 17.3 %collective-permute-start.5 = (bf16[128,512]{1,0:T(8,128)(2,1)S(1)}, bf16[128,512]{1,0:T(8,128)(2,1)S(1)}, u32[]{:S(2)}, u32[]{:S(2)}) collective-permute-start(bf16[128,512]{1,0:T(8,128)(2,1)S(1)} %collective-permute-done.3.refs_5_), channel_id=1, source_target_pairs={{0,8},{4,12},{8,0},{12,4},{16,24},{20,28},{24,16},{28,20},{1,9},{5... | collective-permute-start | bytes 393224 | tf_op jit(solution)/shard_map/ppermute | solution.py:450
  33.2 32.5 %copy-start.4 = (bf16[128,512]{1,0:T(8,128)(2,1)}, bf16[128,512]{1,0:T(8,128)(2,1)S(1)}, u32[]{:S(2)}) copy-start(bf16[128,512]{1,0:T(8,128)(2,1)S(1)} %collective-permute-done.6.refs_8_) | copy-start | bytes 393220
  33.2 13.1 %collective-permute-start.7 = (bf16[128,512]{1,0:T(8,128)(2,1)S(1)}, bf16[128,512]{1,0:T(8,128)(2,1)S(1)}, u32[]{:S(2)}, u32[]{:S(2)}) collective-permute-start(bf16[128,512]{1,0:T(8,128)(2,1)S(1)} %collective-permute-done.6.refs_8_), channel_id=1, source_target_pairs={{0,4},{4,0},{8,12},{12,8},{16,20},{20,16},{24,28},{28,24},{1,5},{5... | collective-permute-start | bytes 393224 | tf_op jit(solution)/shard_map/ppermute | solution.py:450
  39.2 7.7 %collective-permute-start.10 = (bf16[128,512]{1,0:T(8,128)(2,1)}, bf16[128,512]{1,0:T(8,128)(2,1)S(1)}, u32[]{:S(2)}, u32[]{:S(2)}) collective-permute-start(bf16[128,512]{1,0:T(8,128)(2,1)} %project_kv.3.refs_12_), channel_id=1, source_target_pairs={{0,4},{4,0},{8,12},{12,8},{16,20},{20,16},{24,28},{28,24},{1,5},{5... | collective-permute-start | bytes 393224 | tf_op jit(solution)/shard_map/ppermute | solution.py:450
  41.2 24.5 %copy-start.5 = (bf16[128,512]{1,0:T(8,128)(2,1)}, bf16[128,512]{1,0:T(8,128)(2,1)S(1)}, u32[]{:S(2)}) copy-start(bf16[128,512]{1,0:T(8,128)(2,1)S(1)} %collective-permute-done.4.refs_6_) | copy-start | bytes 393220
  41.2 12.0 %collective-permute-start.13 = (bf16[128,512]{1,0:T(8,128)(2,1)}, bf16[128,512]{1,0:T(8,128)(2,1)S(1)}, u32[]{:S(2)}, u32[]{:S(2)}) collective-permute-start(bf16[128,512]{1,0:T(8,128)(2,1)} %project_kv.3.refs_12_), channel_id=1, source_target_pairs={{0,16},{4,20},{8,24},{12,28},{16,0},{20,4},{24,8},{28,12},{1,17},{... | collective-permute-start | bytes 393224 | tf_op jit(solution)/shard_map/ppermute | solution.py:450
  41.2 24.5 %copy-start.6 = (bf16[128,512]{1,0:T(8,128)(2,1)}, bf16[128,512]{1,0:T(8,128)(2,1)S(1)}, u32[]{:S(2)}) copy-start(bf16[128,512]{1,0:T(8,128)(2,1)S(1)} %collective-permute-done.8.refs_10_) | copy-start | bytes 393220
  41.2 12.4 %collective-permute-start.15 = (bf16[128,512]{1,0:T(8,128)(2,1)}, bf16[128,512]{1,0:T(8,128)(2,1)S(1)}, u32[]{:S(2)}, u32[]{:S(2)}) collective-permute-start(bf16[128,512]{1,0:T(8,128)(2,1)} %project_kv.3.refs_12_), channel_id=1, source_target_pairs={{0,24},{4,28},{8,16},{12,20},{16,8},{20,12},{24,0},{28,4},{1,25},{... | collective-permute-start | bytes 393224 | tf_op jit(solution)/shard_map/ppermute | solution.py:450
  45.8 19.8 %collective-permute-start.9 = (bf16[128,512]{1,0:T(8,128)(2,1)S(1)}, bf16[128,512]{1,0:T(8,128)(2,1)S(1)}, u32[]{:S(2)}, u32[]{:S(2)}) collective-permute-start(bf16[128,512]{1,0:T(8,128)(2,1)S(1)} %collective-permute-done.8.refs_10_), channel_id=1, source_target_pairs={{0,4},{4,0},{8,12},{12,8},{16,20},{20,16},{24,28},{28,24},{1,5},{5... | collective-permute-start | bytes 393224 | tf_op jit(solution)/shard_map/ppermute | solution.py:450
  46.3 19.3 %collective-permute-start.11 = (bf16[128,512]{1,0:T(8,128)(2,1)}, bf16[128,512]{1,0:T(8,128)(2,1)S(1)}, u32[]{:S(2)}, u32[]{:S(2)}) collective-permute-start(bf16[128,512]{1,0:T(8,128)(2,1)} %project_kv.3.refs_12_), channel_id=1, source_target_pairs={{0,8},{4,12},{8,0},{12,4},{16,24},{20,28},{24,16},{28,20},{1,9},{5... | collective-permute-start | bytes 393224 | tf_op jit(solution)/shard_map/ppermute | solution.py:450
  46.9 18.7 %collective-permute-start.12 = (bf16[128,512]{1,0:T(8,128)(2,1)S(1)}, bf16[128,512]{1,0:T(8,128)(2,1)S(1)}, u32[]{:S(2)}, u32[]{:S(2)}) collective-permute-start(bf16[128,512]{1,0:T(8,128)(2,1)S(1)} %collective-permute-done.10.refs_13_), channel_id=1, source_target_pairs={{0,8},{4,12},{8,0},{12,4},{16,24},{20,28},{24,16},{28,20},{1,9},{5... | collective-permute-start | bytes 393224 | tf_op jit(solution)/shard_map/ppermute | solution.py:450
  53.1 12.5 %collective-permute-start.14 = (bf16[128,512]{1,0:T(8,128)(2,1)S(1)}, bf16[128,512]{1,0:T(8,128)(2,1)S(1)}, u32[]{:S(2)}, u32[]{:S(2)}) collective-permute-start(bf16[128,512]{1,0:T(8,128)(2,1)S(1)} %collective-permute-done.13.refs_16_), channel_id=1, source_target_pairs={{0,4},{4,0},{8,12},{12,8},{16,20},{20,16},{24,28},{28,24},{1,5},{5... | collective-permute-start | bytes 393224 | tf_op jit(solution)/shard_map/ppermute | solution.py:450
  53.6 12.0 %collective-permute-start.16 = (bf16[128,512]{1,0:T(8,128)(2,1)S(1)}, bf16[128,512]{1,0:T(8,128)(2,1)S(1)}, u32[]{:S(2)}, u32[]{:S(2)}) collective-permute-start(bf16[128,512]{1,0:T(8,128)(2,1)S(1)} %collective-permute-done.15.refs_18_), channel_id=1, source_target_pairs={{0,4},{4,0},{8,12},{12,8},{16,20},{20,16},{24,28},{28,24},{1,5},{5... | collective-permute-start | bytes 393224 | tf_op jit(solution)/shard_map/ppermute | solution.py:450
  75.9 11.0 %collective-permute-start.18 = (bf16[64,4096]{1,0:T(8,128)(2,1)}, bf16[64,4096]{1,0:T(8,128)(2,1)S(1)}, u32[]{:S(2)}, u32[]{:S(2)}) collective-permute-start(bf16[64,4096]{1,0:T(8,128)(2,1)} %get-tuple-element.16), channel_id=1, source_target_pairs={{0,1},{1,0},{2,3},{3,2},{4,5},{5,4},{6,7},{7,6},{8,9},{9,8},{10,11... | collective-permute-start | bytes 1572872 | tf_op jit(solution)/shard_map/ppermute | solution.py:450
  86.4 2.2 %collective-permute-start.17 = (bf16[64,4096]{1,0:T(8,128)(2,1)}, bf16[64,4096]{1,0:T(8,128)(2,1)S(1)}, u32[]{:S(2)}, u32[]{:S(2)}) collective-permute-start(bf16[64,4096]{1,0:T(8,128)(2,1)} %get-tuple-element.14), channel_id=1, source_target_pairs={{0,1},{1,0},{2,3},{3,2},{4,5},{5,4},{6,7},{7,6},{8,9},{9,8},{10,11... | collective-permute-start | bytes 1572872 | tf_op jit(solution)/shard_map/ppermute | solution.py:450
  87.0 14.0 %collective-permute-start.19 = (bf16[64,4096]{1,0:T(8,128)(2,1)S(1)}, bf16[64,4096]{1,0:T(8,128)(2,1)S(1)}, u32[]{:S(2)}, u32[]{:S(2)}) collective-permute-start(bf16[64,4096]{1,0:T(8,128)(2,1)S(1)} %add_convert_fusion.1), channel_id=1, source_target_pairs={{0,2},{1,3},{2,0},{3,1},{4,6},{5,7},{6,4},{7,5},{8,10},{9,11},{10,... | collective-permute-start | bytes 1572872 | tf_op jit(solution)/shard_map/ppermute | solution.py:450
  (14 other events, 117.3 us)
